TPU v7x, 256 devices: a 8x8x2 block of a 8x8x16 slice. The times are simulated.
256 devices in a mesh: sub: 2 (over z), row: 128 (over y, x, core).
Axes of the slice: x: 8, y: 8, z: 2, core: 2. Of those that a mesh axis runs over, the one named last changes fastest.
The devices are a block of a 8x8x16 slice.
Arguments:
- diag_blocks: float32 [4096, 128, 128], P(('sub', 'row')), parts along dimension 0, may hold values from -0.05 to 16, as said below
- coupling: float32 [4096, 3, 128, 128], P(('sub', 'row')), parts along dimension 0, may hold values from -0.05 to 0.05
- offsets: int32 [4096, 3], P(('sub', 'row')), parts along dimension 0, may hold values from 1 to 4, as said below
- mass: float32 [524288], P(('sub', 'row')), parts along dimension 0, may hold values from 0.5 to 2
- initial_modes: float32 [32, 524288], P(None, ('sub', 'row')), parts along dimension 1, may hold values from -6 to 6
Outputs:
- mass_density: float32 [524288], P(('sub', 'row')), parts along dimension 0
- energy_density: float32 [524288], P(('sub', 'row')), parts along dimension 0
There are 2 independent parts, one for each index of `sub`. A program takes and returns all parts, laid end to end along the dimension named above; each array names one. Nothing has to cross between parts.
Inputs may be any that keep to these rules, and one draw needn't show every extreme that they name: `diag_blocks`: each block is symmetric; entries off a block's diagonal lie in -0.05 to 0.05, its diagonal entries in 1 to 16. The 3 offsets of a block row are distinct.
All inputs are finite; a program needn't handle non-finite values.
Results may differ from a plain program's by a relative error of at most 0.0003.
Values sent between devices are 32-bit elements; how exact they have to be, the bound alone decides.
A program may use at most 128 MiB of HBM per device.

v0:
```python
import jax
import jax.numpy as jnp
from jax import lax
from jax.sharding import Mesh
from jax.sharding import PartitionSpec as P

MODES = 32
REACH = 4
ITERS = 3
PURIFY = 28
ROW = ("row_0", "row_1", "row_2")
SUB_ROW = ("sub", "row_0", "row_1", "row_2")


PRECISE = lax.Precision.HIGHEST


def from_behind(value, axis, steps):
    count = lax.axis_size(axis)
    initial, last = (max(0, -steps), min(count, count - steps))
    return lax.ppermute(value, axis, [(source, source + steps) for source in range(initial, last)])


def one_axis_at_a_time(value, axes):
    for axis in axes:
        value = lax.psum(value, axis)
    return value


def one_hot_table(positions, extent):
    return (positions[..., None] == jnp.arange(extent, dtype=jnp.int32)).astype(jnp.float32)


def stiffness_apply(vectors, diag_blocks, coupling, offsets):
    rowcount = vectors.shape[0]
    block_count = diag_blocks.shape[0]
    block_width = diag_blocks.shape[1]
    blocked = vectors.reshape(rowcount, block_count, block_width)
    result = jnp.einsum("nbk,bkj->nbj", blocked, diag_blocks, precision=PRECISE)
    positions = jnp.arange(block_count, dtype=jnp.int32)[:, None] - offsets + REACH
    products = jnp.einsum("nbk,bskj->nbsj", blocked, coupling, precision=PRECISE)
    lower_part = from_behind(vectors[:, (block_count - REACH) * block_width :], ROW, 1)
    extent = block_count + REACH
    extended = jnp.concatenate([lower_part, vectors], axis=1).reshape(rowcount, extent, block_width)
    selector = one_hot_table(positions, extent)
    gathered = jnp.einsum("bse,nek->nbsk", selector, extended, precision=PRECISE)
    result = result + jnp.einsum("nbsk,bsjk->nbj", gathered, coupling, precision=PRECISE)
    spread = jnp.einsum("bse,nbsj->nej", selector, products, precision=PRECISE)
    returned = from_behind(spread[:, :REACH].reshape(rowcount, REACH * block_width), ROW, -1)
    result = result + spread[:, REACH:]
    result = result.at[:, block_count - REACH :].add(returned.reshape(rowcount, REACH, block_width))
    return result.reshape(rowcount, block_count * block_width)


def purify(matrix, occupied, steps_count):
    order = matrix.shape[0]
    identity = jnp.eye(order, dtype=matrix.dtype)
    diagonal = jnp.diagonal(matrix)
    center = jnp.sum(diagonal) / order
    radius = jnp.sum(jnp.abs(matrix), axis=1) - jnp.abs(diagonal)
    highest = jnp.max(diagonal + radius)
    lowest = jnp.min(diagonal - radius)
    factor = jnp.minimum(
        occupied / jnp.maximum(highest - center, 1e-06),
        (order - occupied) / jnp.maximum(center - lowest, 1e-06),
    )
    initial = factor / order * (center * identity - matrix) + occupied / order * identity

    def purify_step(index, density):
        square = jnp.dot(density, density, precision=PRECISE)
        cube = jnp.dot(square, density, precision=PRECISE)
        numerator = jnp.trace(square - cube)
        denominator = jnp.trace(density - square)
        safe_denominator = jnp.where(jnp.abs(denominator) > 1e-12, denominator, 1.0)
        ratio = jnp.clip(numerator / safe_denominator, 0.0, 1.0)
        upward = ((1.0 + ratio) * square - cube) / jnp.maximum(ratio, 0.5)
        downward = ((1.0 - 2.0 * ratio) * density + (1.0 + ratio) * square - cube) / jnp.maximum(
            1.0 - ratio, 0.5
        )
        return jnp.where(ratio >= 0.5, upward, downward)

    return lax.fori_loop(0, steps_count, purify_step, initial)


def ritz_basis(gram_stiff, gram_mass, modes_wanted, steps_count):
    order = gram_stiff.shape[0]
    gram_stiff = 0.5 * (gram_stiff + gram_stiff.T)
    gram_mass = 0.5 * (gram_mass + gram_mass.T)
    scaling = lax.rsqrt(jnp.diagonal(gram_mass) + 1e-06)
    stiff_scaled = scaling[:, None] * gram_stiff * scaling[None, :]
    mass_scaled = scaling[:, None] * gram_mass * scaling[None, :]
    factor_low = jnp.linalg.cholesky(mass_scaled)
    identity = jnp.eye(order, dtype=gram_stiff.dtype)
    inverse_low = lax.linalg.triangular_solve(factor_low, identity, left_side=True, lower=True)
    reduced = jnp.dot(
        jnp.dot(inverse_low, stiff_scaled, precision=PRECISE), inverse_low.T, precision=PRECISE
    )
    reduced = 0.5 * (reduced + reduced.T)
    if order > modes_wanted:
        projector = purify(reduced, modes_wanted, steps_count)
        columns = projector[:, :modes_wanted]
    else:
        columns = identity
    correlation = jnp.dot(columns.T, columns, precision=PRECISE)
    correlation_low = jnp.linalg.cholesky(correlation)
    orthonormal = lax.linalg.triangular_solve(
        correlation_low, columns.T, left_side=True, lower=True
    ).T
    coefficients = scaling[:, None] * jnp.dot(inverse_low.T, orthonormal, precision=PRECISE)
    projected = jnp.dot(
        jnp.dot(orthonormal.T, reduced, precision=PRECISE), orthonormal, precision=PRECISE
    )
    return (coefficients, 0.5 * (projected + projected.T))


def local(diag_blocks, coupling, offsets, mass, initial_modes):
    stiff_diag = jnp.diagonal(diag_blocks, axis1=1, axis2=2).reshape(-1)

    def gram_pair(basis, stiff_basis):
        local_stiff = jnp.dot(basis, stiff_basis.T, precision=PRECISE)
        local_mass = jnp.dot(basis * mass[None, :], basis.T, precision=PRECISE)
        return (one_axis_at_a_time(local_stiff, ROW), one_axis_at_a_time(local_mass, ROW))

    stiff_initial = stiffness_apply(initial_modes, diag_blocks, coupling, offsets)
    gram_stiff, gram_mass = gram_pair(initial_modes, stiff_initial)
    coefficients, projected = ritz_basis(gram_stiff, gram_mass, MODES, PURIFY)
    modes_now = jnp.dot(coefficients.T, initial_modes, precision=PRECISE)
    stiff_modes = jnp.dot(coefficients.T, stiff_initial, precision=PRECISE)
    directions = None
    stiff_directions = None
    for iteration in range(ITERS):
        residual = stiff_modes - jnp.dot(projected, modes_now * mass[None, :], precision=PRECISE)
        precond = residual / stiff_diag[None, :]
        stiff_precond = stiffness_apply(precond, diag_blocks, coupling, offsets)
        if directions is None:
            basis = jnp.concatenate([modes_now, precond], axis=0)
            stiff_basis = jnp.concatenate([stiff_modes, stiff_precond], axis=0)
        else:
            basis = jnp.concatenate([modes_now, precond, directions], axis=0)
            stiff_basis = jnp.concatenate([stiff_modes, stiff_precond, stiff_directions], axis=0)
        gram_stiff, gram_mass = gram_pair(basis, stiff_basis)
        coefficients, projected = ritz_basis(gram_stiff, gram_mass, MODES, PURIFY)
        directions = jnp.dot(coefficients[MODES:].T, basis[MODES:], precision=PRECISE)
        stiff_directions = jnp.dot(coefficients[MODES:].T, stiff_basis[MODES:], precision=PRECISE)
        modes_now = jnp.dot(coefficients.T, basis, precision=PRECISE)
        stiff_modes = jnp.dot(coefficients.T, stiff_basis, precision=PRECISE)
    weight = mass.shape[0] * lax.axis_size(ROW) / MODES
    mass_density = weight * mass * jnp.sum(modes_now * modes_now, axis=0)
    energy_density = weight * jnp.sum(modes_now * stiff_modes, axis=0)
    return (mass_density, energy_density)


def solution(mesh):
    torus = Mesh(
        mesh.devices.reshape(mesh.shape["sub"], 8, 8, 2), ("sub", "row_0", "row_1", "row_2")
    )
    return jax.shard_map(
        local,
        mesh=torus,
        in_specs=(
            P(SUB_ROW, None, None),
            P(SUB_ROW, None, None, None),
            P(SUB_ROW, None),
            P(SUB_ROW),
            P(None, SUB_ROW),
        ),
        out_specs=(P(SUB_ROW), P(SUB_ROW)),
        check_vma=False,
    )
```

profile of v0, /device:TPU:513, one launch (start us, length us, event | category | flops | bytes accessed | tf_op | source)
XLA Modules:
  0.0 1041.2 jit_solution(16284260710776054212)
XLA Ops:
  8.9 4.6 collective-permute-start
  19.0 19.7 %collective-permute-start.1 = (f32[32,512]{1,0:T(8,128)}, f32[32,512]{1,0:T(8,128)}, u32[]{:S(2)}, u32[]{:S(2)}) collective-permute-start(f32[32,512]{1,0:T(8,128)} %copy_bitcast_fusion.10), channel_id=1, source_target_pairs={{1,0},{2,1},{3,2},{4,3},{5,4},{6,5},{7,6},{8,7},{9,8},{10,9},{11,1... | collective-permute-start | bytes 196616 | tf_op jit(solution)/shard_map/ppermute | solution.py:21
  39.3 2.9 cholesky.183
  43.6 2.4 custom-call.44
  46.2 6.0 copy.58
  52.2 2.4 gather_fusion.1
  60.5 3.6 convolution_bitcast_fusion.8
  67.1 20.2 %all-reduce.7 = (f32[32,32]{1,0:T(8,128)S(1)}, f32[32,32]{1,0:T(8,128)S(1)}) all-reduce(f32[32,32]{1,0:T(8,128)S(1)} %fusion.60, f32[32,32]{1,0:T(8,128)S(1)} %convolution_bitcast_fusion.9), channel_id=1, replica_groups=mesh['sub'=2,'row_0'=8,'row_1'=8,'row_2'=2] {'row_0'}, use_global_device_ids=true, to_apply=%region_0.1 | all-reduce | flops 2048 | bytes 16384 | tf_op jit(solution)/shard_map/psum | solution.py:26
  87.3 20.3 %all-reduce.3 = (f32[32,32]{1,0:T(8,128)S(1)}, f32[32,32]{1,0:T(8,128)S(1)}) all-reduce(f32[32,32]{1,0:T(8,128)S(1)} %get-tuple-element.143, f32[32,32]{1,0:T(8,128)S(1)} %get-tuple-element.144), channel_id=1, replica_groups=mesh['sub'=2,'row_0'=8,'row_1'=8,'row_2'=2] {'row_1'}, use_global_device_ids=true, to_apply=%region_1.2 | all-reduce | flops 2048 | bytes 16384 | tf_op jit(solution)/shard_map/psum | solution.py:26
  107.6 16.7 %all-reduce.11 = (f32[32,32]{1,0:T(8,128)S(1)}, f32[32,32]{1,0:T(8,128)S(1)}) all-reduce(f32[32,32]{1,0:T(8,128)S(1)} %get-tuple-element.135, f32[32,32]{1,0:T(8,128)S(1)} %get-tuple-element.136), channel_id=1, replica_groups=mesh['sub'=2,'row_0'=8,'row_1'=8,'row_2'=2] {'row_2'}, use_global_device_ids=true, to_apply=%region_2.3 | all-reduce | flops 2048 | bytes 16384 | tf_op jit(solution)/shard_map/psum | solution.py:26
  125.3 2.9 cholesky.172
  129.5 2.4 custom-call.43
  138.0 2.9 fusion.74
  141.0 2.3 collective-permute-start.2
  154.5 4.6 fusion.17
  161.2 20.8 %all-reduce.6 = (f32[64,64]{1,0:T(8,128)S(1)}, f32[64,64]{1,0:T(8,128)S(1)}) all-reduce(f32[64,64]{1,0:T(8,128)S(1)} %fusion.35, f32[64,64]{1,0:T(8,128)S(1)} %fusion.49), channel_id=1, replica_groups=mesh['sub'=2,'row_0'=8,'row_1'=8,'row_2'=2] {'row_0'}, use_global_device_ids=true, to_apply=%region_8.11 | all-reduce | flops 8192 | bytes 65536 | tf_op jit(solution)/shard_map/psum | solution.py:26
  182.0 23.7 %all-reduce.2 = (f32[64,64]{1,0:T(8,128)S(1)}, f32[64,64]{1,0:T(8,128)}) all-reduce(f32[64,64]{1,0:T(8,128)S(1)} %get-tuple-element.141, f32[64,64]{1,0:T(8,128)S(1)} %get-tuple-element.142), channel_id=1, replica_groups=mesh['sub'=2,'row_0'=8,'row_1'=8,'row_2'=2] {'row_1'}, use_global_device_ids=true, to_apply=%region_9.12 | all-reduce | flops 8192 | bytes 65536 | tf_op jit(solution)/shard_map/psum | solution.py:26
  205.6 19.7 %all-reduce.10 = (f32[64,64]{1,0:T(8,128)S(1)}, f32[64,64]{1,0:T(8,128)S(1)}) all-reduce(f32[64,64]{1,0:T(8,128)S(1)} %get-tuple-element.133, f32[64,64]{1,0:T(8,128)} %get-tuple-element.134), channel_id=1, replica_groups=mesh['sub'=2,'row_0'=8,'row_1'=8,'row_2'=2] {'row_2'}, use_global_device_ids=true, to_apply=%region_10.13 | all-reduce | flops 8192 | bytes 65536 | tf_op jit(solution)/shard_map/psum | solution.py:26
  228.3 5.8 cholesky.60
  235.6 4.9 custom-call.22
  245.7 81.9 %while.34 = (s32[]{:T(128)}, f32[64,64]{1,0:T(8,128)S(1)}, s32[]{:T(128)}, f32[]{:T(128)}, f32[]{:T(128)}, /*index=5*/f32[]{:T(128)}, f32[]{:T(128)}, f32[]{:T(128)}) while((s32[]{:T(128)}, f32[64,64]{1,0:T(8,128)S(1)}, s32[]{:T(128)}, f32[]{:T(128)}, f32[]{:T(128)}, /*index=5*/f32[]{:T(128)}, f32[]{:T(128)}, f32[]{:T(128)}) %tuple.100), condition=%wide.region_23.26_spmd, body=%wide.region_20.25_spmd.sunk | while | flops 6352909 | bytes 147713 | solution.py:82
  327.9 2.9 cholesky.194
  332.1 2.4 custom-call.23
  341.7 3.0 fusion.71
  347.2 2.5 collective-permute-start.4
  359.4 4.6 fusion.14
  367.2 75.7 %all-reduce.25.cloned.1.call-done = (f32[96,96]{1,0:T(8,128)}, f32[96,96]{1,0:T(8,128)}) async-done(((f32[96,96]{1,0:T(8,128)}, f32[96,96]{1,0:T(8,128)}), (f32[96,96]{1,0:T(8,128)}, f32[96,96]{1,0:T(8,128)})) %all-reduce.25.cloned.1.call-update) | async-done | bytes 73744 | tf_op jit(solution)/shard_map/psum | solution.py:26
  443.1 75.6 %all-reduce.21.cloned.1.call-done = (f32[96,96]{1,0:T(8,128)}, f32[96,96]{1,0:T(8,128)}) async-done(((f32[96,96]{1,0:T(8,128)}, f32[96,96]{1,0:T(8,128)}), (f32[96,96]{1,0:T(8,128)}, f32[96,96]{1,0:T(8,128)})) %all-reduce.21.cloned.1.call-update) | async-done | bytes 73744 | tf_op jit(solution)/shard_map/psum | solution.py:26
  518.8 38.9 %all-reduce.29.cloned.1.call-done = (f32[96,96]{1,0:T(8,128)}, f32[96,96]{1,0:T(8,128)}) async-done(((f32[96,96]{1,0:T(8,128)}, f32[96,96]{1,0:T(8,128)}), (f32[96,96]{1,0:T(8,128)}, f32[96,96]{1,0:T(8,128)})) %all-reduce.29.cloned.1.call-update) | async-done | bytes 73744 | tf_op jit(solution)/shard_map/psum | solution.py:26
  561.8 8.8 cholesky.205
  571.9 7.4 custom-call.45
  586.0 89.0 %while.35 = (s32[]{:T(128)}, f32[96,96]{1,0:T(8,128)S(1)}, s32[]{:T(128)}, f32[]{:T(128)}, f32[]{:T(128)}, /*index=5*/f32[]{:T(128)}, f32[]{:T(128)}, f32[]{:T(128)}) while((s32[]{:T(128)}, f32[96,96]{1,0:T(8,128)S(1)}, s32[]{:T(128)}, f32[]{:T(128)}, f32[]{:T(128)}, /*index=5*/f32[]{:T(128)}, f32[]{:T(128)}, f32[]{:T(128)}) %tuple.103), condition=%wide.region_39.44_spmd, body=%wide.region_36.43_spmd.sunk | while | flops 21371904 | bytes 332033 | solution.py:82
  676.0 3.6 cholesky.216
  681.0 2.4 custom-call.46
  684.9 2.3 fusion.64
  687.2 2.3 fusion.38
  691.3 3.0 fusion.68
  694.3 2.1 fusion.44
  696.9 2.6 collective-permute-start.6
  709.9 4.6 fusion.11
  717.6 73.0 %all-reduce.23.cloned.1.call-done = (f32[96,96]{1,0:T(8,128)}, f32[96,96]{1,0:T(8,128)}) async-done(((f32[96,96]{1,0:T(8,128)}, f32[96,96]{1,0:T(8,128)}), (f32[96,96]{1,0:T(8,128)}, f32[96,96]{1,0:T(8,128)})) %all-reduce.23.cloned.1.call-update) | async-done | bytes 73744 | tf_op jit(solution)/shard_map/psum | solution.py:26
  791.1 75.2 %all-reduce.19.cloned.1.call-done = (f32[96,96]{1,0:T(8,128)}, f32[96,96]{1,0:T(8,128)}) async-done(((f32[96,96]{1,0:T(8,128)}, f32[96,96]{1,0:T(8,128)}), (f32[96,96]{1,0:T(8,128)}, f32[96,96]{1,0:T(8,128)})) %all-reduce.19.cloned.1.call-update) | async-done | bytes 73744 | tf_op jit(solution)/shard_map/psum | solution.py:26
  866.4 38.8 %all-reduce.27.cloned.1.call-done = (f32[96,96]{1,0:T(8,128)}, f32[96,96]{1,0:T(8,128)}) async-done(((f32[96,96]{1,0:T(8,128)}, f32[96,96]{1,0:T(8,128)}), (f32[96,96]{1,0:T(8,128)}, f32[96,96]{1,0:T(8,128)})) %all-reduce.27.cloned.1.call-update) | async-done | bytes 73744 | tf_op jit(solution)/shard_map/psum | solution.py:26
  909.8 9.6 cholesky.227
  920.7 8.0 custom-call.47
  937.8 83.4 %while.36 = (s32[]{:T(128)}, f32[96,96]{1,0:T(8,128)S(1)}, s32[]{:T(128)}, f32[]{:T(128)}, f32[]{:T(128)}, /*index=5*/f32[]{:T(128)}, f32[]{:T(128)}, f32[]{:T(128)}) while((s32[]{:T(128)}, f32[96,96]{1,0:T(8,128)S(1)}, s32[]{:T(128)}, f32[]{:T(128)}, f32[]{:T(128)}, /*index=5*/f32[]{:T(128)}, f32[]{:T(128)}, f32[]{:T(128)}) %tuple.106), condition=%wide.region_53.59_spmd, body=%wide.region_50.58_spmd.sunk | while | flops 21371904 | bytes 332033 | solution.py:82
  1021.5 2.9 cholesky.238
  1025.7 2.4 custom-call.48
  (549 shorter events, 206.6 us)
Async XLA Ops:
  7.2 8.0 copy-start
  7.2 435.7 %all-reduce.25.cloned.1.call-start = ((), (), s32[]{:S(2)}) async-start(), calls=%async_computation.3 | async-start | bytes 196608 | tf_op jit(solution)/shard_map/psum | solution.py:26
  8.9 46.7 %collective-permute-start = (f32[32,512]{1,0:T(8,128)}, f32[32,512]{1,0:T(8,128)}, u32[]{:S(2)}, u32[]{:S(2)}) collective-permute-start(f32[32,512]{1,0:T(8,128)} %slice.181), channel_id=1, source_target_pairs={{0,1},{1,2},{2,3},{3,4},{4,5},{5,6},{6,7},{7,8},{8,9},{9,10},{10,1... | collective-permute-start | bytes 196616 | tf_op jit(solution)/shard_map/ppermute | solution.py:21
  14.2 687.6 %copy-start.37 = (s32[16,3]{0,1:T(4,128)}, s32[16,3]{0,1:T(4,128)S(1)}, u32[]{:S(2)}) copy-start(s32[16,3]{0,1:T(4,128)S(1)} %subtract_add_fusion) | copy-start | bytes 580
  15.2 23.7 %copy-start.2 = (f32[32,2048]{1,0:T(8,128)S(1)}, f32[32,2048]{1,0:T(8,128)}, u32[]{:S(2)}) copy-start(f32[32,2048]{1,0:T(8,128)} %param.31) | copy-start | bytes 786436
  15.2 23.7 %copy-start.38 = (f32[2048]{0:T(1024)S(1)}, f32[2048]{0:T(1024)}, u32[]{:S(2)}) copy-start(f32[2048]{0:T(1024)} %param.30) | copy-start | bytes 24580
  18.3 20.4 %copy-start.22 = (f32[32,128,20]{1,0,2:T(8,128)}, f32[32,128,20]{1,0,2:T(8,128)S(1)}, u32[]{:S(2)}) copy-start(f32[32,128,20]{1,0,2:T(8,128)S(1)} %copy.223) | copy-start | bytes 983044
  19.0 46.2 %collective-permute-start.1 = (f32[32,512]{1,0:T(8,128)}, f32[32,512]{1,0:T(8,128)}, u32[]{:S(2)}, u32[]{:S(2)}) collective-permute-start(f32[32,512]{1,0:T(8,128)} %copy_bitcast_fusion.10), channel_id=1, source_target_pairs={{1,0},{2,1},{3,2},{4,3},{5,4},{6,5},{7,6},{8,7},{9,8},{10,9},{11,1... | collective-permute-start | bytes 196616 | tf_op jit(solution)/shard_map/ppermute | solution.py:21
  55.5 81.0 %copy-start.39 = (f32[16,128]{1,0:T(8,128)}, f32[16,128]{1,0:T(8,128)S(1)}, u32[]{:S(2)}) copy-start(f32[16,128]{1,0:T(8,128)S(1)} %copy.59) | copy-start | bytes 24580
  58.9 5.2 copy-start.1
  58.9 5.2 copy-start.23
  141.0 9.4 collective-permute-start.2
  143.3 4.4 copy-start.6
  148.3 10.8 %collective-permute-start.3 = (f32[32,512]{1,0:T(8,128)}, f32[32,512]{1,0:T(8,128)S(1)}, u32[]{:S(2)}, u32[]{:S(2)}) collective-permute-start(f32[32,512]{1,0:T(8,128)} %copy_bitcast_fusion.9), channel_id=1, source_target_pairs={{1,0},{2,1},{3,2},{4,3},{5,4},{6,5},{7,6},{8,7},{9,8},{10,9},{11,1... | collective-permute-start | bytes 196616 | tf_op jit(solution)/shard_map/ppermute | solution.py:21
  152.9 7.7 copy-start.7
  152.9 7.7 copy-start.16
  341.7 15.4 %copy-start.3 = (f32[32,2048]{1,0:T(8,128)}, f32[32,2048]{1,0:T(8,128)S(1)}, u32[]{:S(2)}) copy-start(f32[32,2048]{1,0:T(8,128)S(1)} %fusion.1) | copy-start | bytes 786436
  347.2 8.4 copy-start.12
  347.2 9.8 collective-permute-start.4
  349.8 5.9 copy-start.25
  352.8 4.2 copy-start.21
  353.5 10.5 %collective-permute-start.5 = (f32[32,512]{1,0:T(8,128)}, f32[32,512]{1,0:T(8,128)}, u32[]{:S(2)}, u32[]{:S(2)}) collective-permute-start(f32[32,512]{1,0:T(8,128)} %copy_bitcast_fusion.8), channel_id=1, source_target_pairs={{1,0},{2,1},{3,2},{4,3},{5,4},{6,5},{7,6},{8,7},{9,8},{10,9},{11,1... | collective-permute-start | bytes 196616 | tf_op jit(solution)/shard_map/ppermute | solution.py:21
  358.8 6.8 copy-start.4
  358.9 6.8 copy-start.13
  358.9 6.8 copy-start.15
  358.9 6.8 copy-start.26
  358.9 6.8 copy-start.27
  367.1 151.6 %all-reduce.21.cloned.1.call-start = ((), (), s32[]{:S(2)}) async-start(), calls=%async_computation.1 | async-start | bytes 196608 | tf_op jit(solution)/shard_map/psum | solution.py:26
  443.0 114.8 %all-reduce.29.cloned.1.call-start = ((), (), s32[]{:S(2)}) async-start(), calls=%async_computation.5 | async-start | bytes 196608 | tf_op jit(solution)/shard_map/psum | solution.py:26
  518.8 271.9 %all-reduce.23.cloned.1.call-start = ((), (), s32[]{:S(2)}) async-start(), calls=%async_computation.2 | async-start | bytes 196608 | tf_op jit(solution)/shard_map/psum | solution.py:26
  560.8 25.3 %copy-start.42 = (f32[96]{0:T(128)}, f32[96]{0:T(128)S(1)}, u32[]{:S(2)}) copy-start(f32[96]{0:T(128)S(1)} %get-tuple-element.165) | copy-start | bytes 1156
  579.5 2.2 copy-start.35
  675.0 21.4 %copy-start.5 = (f32[32,2048]{1,0:T(8,128)S(1)}, f32[32,2048]{1,0:T(8,128)}, u32[]{:S(2)}) copy-start(f32[32,2048]{1,0:T(8,128)} %copy-done.3) | copy-start | bytes 786436
  689.8 6.7 copy-start.14
  691.3 16.1 %copy-start.8 = (f32[32,2048]{1,0:T(8,128)}, f32[32,2048]{1,0:T(8,128)S(1)}, u32[]{:S(2)}) copy-start(f32[32,2048]{1,0:T(8,128)S(1)} %fusion) | copy-start | bytes 786436
  696.9 9.1 copy-start.28
  696.9 10.5 %collective-permute-start.6 = (f32[32,512]{1,0:T(8,128)S(1)}, f32[32,512]{1,0:T(8,128)S(1)}, u32[]{:S(2)}, u32[]{:S(2)}) collective-permute-start(f32[32,512]{1,0:T(8,128)S(1)} %slice.231), channel_id=1, source_target_pairs={{0,1},{1,2},{2,3},{3,4},{4,5},{5,6},{6,7},{7,8},{8,9},{9,10},{10,1... | collective-permute-start | bytes 196616 | tf_op jit(solution)/shard_map/ppermute | solution.py:21
  699.6 6.4 copy-start.32
  704.0 10.5 %collective-permute-start.7 = (f32[32,512]{1,0:T(8,128)}, f32[32,512]{1,0:T(8,128)}, u32[]{:S(2)}, u32[]{:S(2)}) collective-permute-start(f32[32,512]{1,0:T(8,128)} %copy_bitcast_fusion.7), channel_id=1, source_target_pairs={{1,0},{2,1},{3,2},{4,3},{5,4},{6,5},{7,6},{8,7},{9,8},{10,9},{11,1... | collective-permute-start | bytes 196616 | tf_op jit(solution)/shard_map/ppermute | solution.py:21
  708.2 7.9 copy-start.9
  708.2 7.9 copy-start.24
  708.2 7.9 copy-start.29
  708.2 7.9 copy-start.31
  708.2 7.9 copy-start.33
  717.6 148.7 %all-reduce.19.cloned.1.call-start = ((), (), s32[]{:S(2)}) async-start(), calls=%async_computation | async-start | bytes 196608 | tf_op jit(solution)/shard_map/psum | solution.py:26
  790.7 114.5 %all-reduce.27.cloned.1.call-start = ((), (), s32[]{:S(2)}) async-start(), calls=%async_computation.4 | async-start | bytes 196608 | tf_op jit(solution)/shard_map/psum | solution.py:26
  908.2 29.5 %copy-start.40 = (f32[96]{0:T(128)}, f32[96]{0:T(128)S(1)}, u32[]{:S(2)}) copy-start(f32[96]{0:T(128)S(1)} %get-tuple-element.163) | copy-start | bytes 1156
  929.8 2.3 copy-start.34
  (10 other events, 7.4 us)
Sparse Core Ops, SparseCore 0:
  367.2 75.6 all-reduce.24
  445.4 73.2 all-reduce.20
  521.3 36.3 all-reduce.28
  717.7 72.9 all-reduce.22
  793.0 73.2 all-reduce.18
  868.8 36.3 all-reduce.26
where the time goes:
time: 1050 us; the launch traced here: 1040 us
  waiting for transfers between devices  378 us (36%)
  matrix products  173 us (16%)
  loops' own time  168 us (16%)
  blocking collectives  121 us (12%)
  other arithmetic  101 us (10%)
  local copies, waits for them, and re-layouts  39.7 us (4%)
  starting transfers between devices  38.4 us (4%)
  between operations  22.1 us (2%)
    psum x6, waiting for transfers between devices, one_axis_at_a_time(): value = lax.psum(value, axis)  377 us
    another operation x3, loops' own time, purify(): return lax.fori_loop(0, steps_count, purify_step, initial)  168 us
    psum x6, blocking collectives, one_axis_at_a_time(): value = lax.psum(value, axis)  121 us
    dot_general x84, matrix products, purify_step(): cube = jnp.dot(square, density, precision=PRECISE)  69.6 us
    ppermute x8, starting transfers between devices, from_behind(): lax.ppermute(value, axis, [(source, source + steps) for source in range(i...  37.8 us
    another operation x12, other arithmetic, ritz_basis(): factor_low = jnp.linalg.cholesky(mass_scaled)  30 us
    another operation x8, other arithmetic, ritz_basis(): lax.linalg.triangular_solve(factor_low, identity, left_side=True, lower=T...  25.2 us
  transfers between devices with their start and end apart: 14, of which 6 were waited for; matrix products, arithmetic and copies ran while one was open for 7% of the time, Pallas kernels for 0%

commit v1 on v0

v1 whole, which is shorter than its diff:
```python
import jax
import jax.numpy as jnp
from jax import lax
from jax.experimental import pallas as pl
from jax.experimental.pallas import tpu as pltpu
from jax.sharding import PartitionSpec as P

MODES = 32
REACH = 4
SLOTS = 3
ITERS = 3
PURIFY = 28
WIDTH = 128
TORUS = (8, 8, 2)
MESH = pl.DeviceIdType.MESH

HIGH = lax.Precision.HIGH
HIGHEST = lax.Precision.HIGHEST


def mm(a, b, precision):
    return lax.dot_general(
        a, b, (((1,), (0,)), ((), ())), precision=precision, preferred_element_type=jnp.float32
    )


def mm_nt(a, b, precision):
    return lax.dot_general(
        a, b, (((1,), (1,)), ((), ())), precision=precision, preferred_element_type=jnp.float32
    )


def lanes(shape):
    return lax.broadcasted_iota(jnp.int32, shape, 1)


def sublanes(shape):
    return lax.broadcasted_iota(jnp.int32, shape, 0)


def eye(n):
    return (sublanes((n, n)) == lanes((n, n))).astype(jnp.float32)


def total(x):
    return jnp.sum(jnp.sum(x, axis=0, keepdims=True), axis=1, keepdims=True)


def inverse_factor(table, first):
    rows, cols = table.shape
    done = []
    for start in range(0, rows, 8):
        live = table.shape[0]
        column = [
            jnp.broadcast_to(table[:, first + start + k : first + start + k + 1], (live, cols))
            for k in range(8)
        ]
        index = sublanes((live, cols))
        lane = lanes((live, cols))
        for k in range(8):
            at = first + start + k
            pivot = column[k][k : k + 1, :]
            scale = lax.rsqrt(pivot)
            row = jnp.where(lane[0:1] == at, 1.0, table[k : k + 1, :]) * scale
            factor = jnp.where(index > k, column[k] * scale, 0.0)
            table = jnp.where((index > k) & (lane == at), 0.0, table) - factor * row
            table = jnp.where(index == k, row, table)
            for m in range(k + 1, 8):
                column[m] = column[m] - factor * (column[m][k : k + 1, :] * scale)
        done.append(table[:8])
        table = table[8:]
    result = jnp.concatenate(done, axis=0) if len(done) > 1 else done[0]
    shape = (rows, cols)
    return jnp.where(lanes(shape) <= sublanes(shape) + first, result, 0.0)


def purify(matrix):
    n = matrix.shape[0]
    identity = eye(n)
    diagonal = jnp.sum(matrix * identity, axis=0, keepdims=True)
    radius = jnp.sum(jnp.abs(matrix), axis=0, keepdims=True) - jnp.abs(diagonal)
    center = jnp.sum(diagonal, axis=1, keepdims=True) / n
    highest = jnp.max(diagonal + radius, axis=1, keepdims=True)
    lowest = jnp.min(diagonal - radius, axis=1, keepdims=True)
    factor = jnp.minimum(
        MODES / jnp.maximum(highest - center, 1e-6), (n - MODES) / jnp.maximum(center - lowest, 1e-6)
    )
    initial = factor / n * (center * identity - matrix) + MODES / n * identity

    def step(index, density):
        square = mm(density, density, HIGHEST)
        cube = mm(square, density, HIGHEST)
        denominator = total((density - square) * identity)
        numerator = total(square * (identity - density))
        safe = jnp.where(jnp.abs(denominator) > 1e-12, denominator, 1.0)
        ratio = jnp.clip(numerator / safe, 0.0, 1.0)
        up = ratio >= 0.5
        scale = 1.0 / jnp.maximum(jnp.where(up, ratio, 1.0 - ratio), 0.5)
        first = jnp.where(up, 0.0, (1.0 - 2.0 * ratio) * scale)
        second = (1.0 + ratio) * scale
        return first * density + second * square - scale * cube

    return lax.fori_loop(0, PURIFY, step, initial)


def scaled(gram_stiff, gram_mass):
    n = gram_stiff.shape[0]
    masked = gram_mass * eye(n)
    across = lax.rsqrt(jnp.sum(masked, axis=0, keepdims=True) + 1e-6)
    down = lax.rsqrt(jnp.sum(masked, axis=1, keepdims=True) + 1e-6)
    return across, gram_stiff * down * across, gram_mass * down * across


def ritz_first(gram_stiff, gram_mass):
    gram_stiff = 0.5 * (gram_stiff + gram_stiff.T)
    gram_mass = 0.5 * (gram_mass + gram_mass.T)
    across, stiff, mass = scaled(gram_stiff, gram_mass)
    inverse = inverse_factor(mass, 0)
    reduced = mm_nt(mm(inverse, stiff, HIGHEST), inverse, HIGHEST)
    return inverse * across, 0.5 * (reduced + reduced.T)


def ritz_next(gram_stiff, gram_mass):
    n = gram_stiff.shape[0]
    rest = n - MODES
    across, stiff, mass = scaled(gram_stiff, gram_mass)
    lead = 1.0 + 1e-6
    side = mass[:, :MODES]
    side = jnp.where(sublanes((n, MODES)) < MODES, 0.0, side)
    lower = mass[MODES:, :]
    schur = lower - lead * mm_nt(side[MODES:], side, HIGHEST)
    lane = lanes((rest, n))
    bottom = inverse_factor(jnp.where(lane < MODES, -lead * lower, schur), MODES)
    shape = (MODES, n)
    unit = jnp.where(lanes(shape) == sublanes(shape), 1.0, 0.0)
    inverse = jnp.concatenate([lead**0.5 * unit, bottom], axis=0)
    reduced = mm_nt(mm(inverse, stiff, HIGHEST), inverse, HIGHEST)
    reduced = 0.5 * (reduced + reduced.T)
    rows = purify(reduced)[:MODES]
    change = inverse_factor(mm_nt(rows, rows, HIGHEST), 0)
    rows = mm(change, rows, HIGHEST)
    coefficients = mm(rows, inverse, HIGHEST) * across
    padded = jnp.concatenate([rows, jnp.zeros((rest, n), jnp.float32)], axis=0)
    projected = mm_nt(mm(rows, reduced, HIGHEST), padded, HIGHEST)
    return coefficients, projected


def solve_kernel(
    sizes,
    diag,
    coupling,
    offsets,
    slot_of,
    mass,
    initial,
    mass_out,
    energy_out,
    inverse_diag,
    product,
    ext0,
    ext1,
    ext2,
    ext3,
    stiff_new,
    modes,
    stiff_modes,
    direction,
    stiff_direction,
    edge,
    landing,
    returned,
    part,
    swapped,
    slots,
    summed,
    halo_send,
    halo_recv,
    swap_send,
    swap_recv,
    ring_send,
    ring_recv,
):
    count, blocks = sizes
    ny, nx, cores = TORUS
    side = nx
    me = lax.axis_index("row")
    core = me % cores
    x = (me // cores) % nx
    y = me // (cores * nx)
    partner = me + 1 - 2 * core
    exts = (ext0, ext1, ext2, ext3)

    def peer(phase, k):
        along_x = (1 - core) if phase == 0 else core
        px = (x + k * along_x) % nx
        py = (y + k * (1 - along_x)) % ny
        return (py * nx + px) * cores + core

    def place(phase):
        along_x = (1 - core) if phase == 0 else core
        return x * along_x + y * (1 - along_x)

    barrier = pltpu.get_barrier_semaphore()
    pl.semaphore_signal(barrier, inc=1, device_id={"row": partner}, device_id_type=MESH)
    for phase in range(2):
        for k in range(1, side):
            pl.semaphore_signal(barrier, inc=1, device_id={"row": peer(phase, k)}, device_id_type=MESH)

    for neighbour in ((me + 1) % count, (me + count - 1) % count):
        pl.semaphore_signal(barrier, inc=1, device_id={"row": neighbour}, device_id_type=MESH)

    def forward(app):
        return pltpu.make_async_remote_copy(
            src_ref=exts[app].at[pl.ds(blocks, REACH)],
            dst_ref=landing.at[app],
            send_sem=halo_send.at[app, 0],
            recv_sem=halo_recv.at[app, 0],
            device_id={"row": me + 1},
            device_id_type=MESH,
        )

    def backward(app):
        return pltpu.make_async_remote_copy(
            src_ref=edge.at[app],
            dst_ref=returned.at[app],
            send_sem=halo_send.at[app, 1],
            recv_sem=halo_recv.at[app, 1],
            device_id={"row": me - 1},
            device_id_type=MESH,
        )

    def own_products(ext, b):
        weights = jnp.concatenate([diag[b]] + [coupling[b, s] for s in range(SLOTS)], axis=1)
        out = mm(ext[b + REACH], weights, HIGH)
        stiff_new[b] = out[:, :WIDTH]
        for s in range(SLOTS):
            product[b, s] = out[:, (s + 1) * WIDTH : (s + 2) * WIDTH]

    def gathered_products(ext, b):
        taken = jnp.concatenate(
            [ext[b + REACH - offsets[b, s]] for s in range(SLOTS)], axis=1
        )
        weights = jnp.concatenate([coupling[b, s] for s in range(SLOTS)], axis=1)
        return mm_nt(taken, weights, HIGH)

    def apply_stiffness(app, wait_entry):
        ext = exts[app]
        for b in range(REACH):
            own_products(ext, b)
        for e in range(REACH):
            out = jnp.zeros((MODES, WIDTH), jnp.float32)
            for b in range(e + 1):
                out = out + product[b, slot_of[b, b - e + REACH - 1]]
            edge[app, e] = out
        wait_entry()

        @pl.when(me < count - 1)
        def _():
            forward(app).start()

        @pl.when(me > 0)
        def _():
            backward(app).start()

        @pl.loop(1, blocks // REACH)
        def _(group):
            for k in range(REACH):
                own_products(ext, group * REACH + k)

        def spread(b):
            return product[b + 1, slot_of[b + 1, 0]], product[b + 2, slot_of[b + 2, 1]], product[
                b + 3, slot_of[b + 3, 2]], product[b + 4, slot_of[b + 4, 3]]

        @pl.loop(1, blocks // REACH)
        def _(group):
            for k in range(REACH):
                b = group * REACH + k
                d0, d1, d2, d3 = spread(b)
                stiff_new[b] = stiff_new[b] + gathered_products(ext, b) + ((d0 + d1) + (d2 + d3))

        @pl.when(me > 0)
        def _():
            forward(app).wait_recv()
            ext[0:REACH] = landing[app]

        @pl.when(me == 0)
        def _():
            ext[0:REACH] = jnp.zeros((REACH, MODES, WIDTH), jnp.float32)

        for b in range(REACH):
            d0, d1, d2, d3 = spread(b)
            stiff_new[b] = stiff_new[b] + gathered_products(ext, b) + ((d0 + d1) + (d2 + d3))

        @pl.when(me < count - 1)
        def _():
            backward(app).wait_recv()
            for k in range(REACH):
                b = blocks - REACH + k
                stiff_new[b] = stiff_new[b] + returned[app, k]

        @pl.when(me < count - 1)
        def _():
            forward(app).wait_send()

        @pl.when(me > 0)
        def _():
            backward(app).wait_send()

    def swap(app, stage):
        if stage == 0:
            source, target = part.at[app, 1 - core], swapped.at[app]
        else:
            source, target = summed.at[app, core], summed.at[app, core]
        return pltpu.make_async_remote_copy(
            src_ref=source,
            dst_ref=target,
            send_sem=swap_send.at[app, stage],
            recv_sem=swap_recv.at[app, stage],
            device_id={"row": partner},
            device_id_type=MESH,
        )

    def ring(app, phase, k, slot):
        return pltpu.make_async_remote_copy(
            src_ref=slots.at[app, phase, slot],
            dst_ref=slots.at[app, phase, slot],
            send_sem=ring_send.at[app, phase, k],
            recv_sem=ring_recv.at[app, phase, slot],
            device_id={"row": peer(phase, k)},
            device_id_type=MESH,
        )

    def sum_start(app):
        swap(app, 0).start()

    def sum_finish(app):
        swap(app, 0).wait_recv()
        value = part[app, core] + swapped[app]
        for phase in range(2):
            mine = place(phase)
            slots[app, phase, mine] = value
            for k in range(1, side):
                ring(app, phase, k, mine).start()
            for k in range(1, side):
                ring(app, phase, k, (mine + k) % side).wait_recv()
            value = slots[app, phase, 0]
            for k in range(1, side):
                value = value + slots[app, phase, k]
        summed[app, core] = value
        swap(app, 1).start()
        pltpu.make_async_remote_copy(
            src_ref=summed.at[app, core],
            dst_ref=summed.at[app, 1 - core],
            send_sem=swap_send.at[app, 1],
            recv_sem=swap_recv.at[app, 1],
            device_id={"row": partner},
            device_id_type=MESH,
        ).wait_recv()
        stiff, mass_part = summed[app, 0], summed[app, 1]
        swap(app, 0).wait_send()
        swap(app, 1).wait_send()
        for phase in range(2):
            for k in range(1, side):
                ring(app, phase, k, place(phase)).wait_send()
        return stiff, mass_part

    def wait_barrier():
        pl.semaphore_wait(barrier, 3 + 2 * (side - 1))

    def wide(refs, pieces, group):
        return jnp.concatenate(
            [jnp.concatenate([ref[group * pieces + k + shift] for ref, shift in refs], axis=0)
             for k in range(pieces)], axis=1)

    def mass_wide(pieces, group):
        return jnp.concatenate([mass[pl.ds(group * pieces + k, 1), :] for k in range(pieces)], axis=1)

    def grams(app, basis, stiff_basis):
        ext = exts[app]
        order = MODES * len(basis)
        pieces = 4

        def body(group, carry):
            left = wide([(ext, REACH)], pieces, group)
            return (
                carry[0] + mm_nt(left, wide(stiff_basis, pieces, group), HIGH),
                carry[1] + mm_nt(left * mass_wide(pieces, group), wide(basis, pieces, group), HIGH),
            )

        zero = jnp.zeros((MODES, order), jnp.float32)
        stiff, weighted = lax.fori_loop(0, blocks // pieces, body, (zero, zero))
        part[app] = jnp.zeros((2, MODES, WIDTH), jnp.float32)
        part[app, 0, :, 0:order] = stiff
        part[app, 1, :, 0:order] = weighted

    identity = eye(WIDTH)

    @pl.loop(0, blocks)
    def _(b):
        inverse_diag[pl.ds(b, 1), :] = 1.0 / jnp.sum(diag[b] * identity, axis=0, keepdims=True)

    @pl.loop(0, blocks + REACH)
    def _(b):
        product[b, SLOTS] = jnp.zeros((MODES, WIDTH), jnp.float32)

    for b in range(blocks):
        ext0[b + REACH] = initial[:, b * WIDTH : (b + 1) * WIDTH]
    apply_stiffness(0, wait_barrier)
    grams(0, [(ext0, REACH)], [(stiff_new, 0)])
    sum_start(0)
    gram_stiff, gram_mass = sum_finish(0)
    coefficients, projected = ritz_first(gram_stiff[:, :MODES], gram_mass[:, :MODES])
    lead_stiff = projected
    basis, stiff_basis = [(ext0, REACH)], [(stiff_new, 0)]
    previous = None

    for step in range(1, ITERS + 1):
        ext = exts[step]
        order = coefficients.shape[1]
        shape = (MODES, order)
        later = jnp.where(lanes(shape) < MODES, 0.0, coefficients)
        both = coefficients if previous is None else jnp.concatenate([coefficients, later], axis=0)

        def update(group, pieces, basis=basis, stiff_basis=stiff_basis, both=both, ext=ext,
                   projected=projected):
            new = mm(both, wide(basis, pieces, group), HIGH)
            stiff = mm(both, wide(stiff_basis, pieces, group), HIGH)
            weighted = new[:MODES] * mass_wide(pieces, group)
            scale = jnp.concatenate(
                [inverse_diag[pl.ds(group * pieces + k, 1), :] for k in range(pieces)], axis=1)
            residual = (stiff[:MODES] - mm(projected[:, :MODES], weighted, HIGH)) * scale
            for k in range(pieces):
                b = group * pieces + k
                cut = slice(k * WIDTH, (k + 1) * WIDTH)
                modes[b] = new[:MODES, cut]
                stiff_modes[b] = stiff[:MODES, cut]
                ext[b + REACH] = residual[:, cut]
                if both.shape[0] > MODES:
                    direction[b] = new[MODES:, cut]
                    stiff_direction[b] = stiff[MODES:, cut]

        @pl.loop(0, blocks // 4)
        def _(group):
            update(group, 4)

        apply_stiffness(step, lambda: None)
        basis = [(modes, 0), (ext, REACH)]
        stiff_basis = [(stiff_modes, 0), (stiff_new, 0)]
        if previous is not None:
            basis.append((direction, 0))
            stiff_basis.append((stiff_direction, 0))
        grams(step, basis, stiff_basis)
        sum_start(step)
        n = MODES * len(basis)
        shape = (MODES, n)
        lane = lanes(shape)
        unit = jnp.where(lane == sublanes(shape), 0.5, 0.0)
        if previous is None:
            placed = mm(0.5 * lead_stiff, jnp.where(lane == sublanes(shape), 1.0, 0.0), HIGHEST)
            third = None
        else:
            placed = projected
            if placed.shape[1] < n:
                grown = jnp.where(lane == sublanes(shape), 1.0, 0.0)
                placed = mm(placed[:, :MODES], grown, HIGHEST)
            placed = 0.5 * placed
            zero = jnp.zeros((MODES, order), jnp.float32)
            spread_rows = jnp.concatenate([coefficients, zero, later], axis=0)
            third = [
                mm_nt(mm(later, old, HIGHEST), spread_rows, HIGHEST)
                * jnp.where(lane < 2 * MODES, 1.0, 0.5)
                for old in previous
            ]
        summed_stiff, summed_mass = sum_finish(step)
        half = jnp.where((lane >= MODES) & (lane < 2 * MODES), 0.5, 1.0)
        rows = [[placed, summed_stiff[:, :n] * half], [unit, summed_mass[:, :n] * half]]
        if third is not None:
            rows[0].append(third[0])
            rows[1].append(third[1])
        full = [jnp.concatenate(r, axis=0) for r in rows]
        full = [f + f.T for f in full]
        coefficients, projected = ritz_next(full[0], full[1])
        previous = full

    weight = count * blocks * WIDTH / MODES

    @pl.loop(0, blocks // 4)
    def _(group):
        new = mm(coefficients, wide(basis, 4, group), HIGH)
        stiff = mm(coefficients, wide(stiff_basis, 4, group), HIGH)
        density = weight * jnp.sum(new * new, axis=0, keepdims=True) * mass_wide(4, group)
        energy = weight * jnp.sum(new * stiff, axis=0, keepdims=True)
        for k in range(4):
            cut = slice(k * WIDTH, (k + 1) * WIDTH)
            mass_out[pl.ds(group * 4 + k, 1), :] = density[:, cut]
            energy_out[pl.ds(group * 4 + k, 1), :] = energy[:, cut]


def solution(mesh):
    count = mesh.shape["row"]

    def local(diag_blocks, coupling, offsets, mass, initial_modes):
        blocks = diag_blocks.shape[0]
        apps = ITERS + 1
        side = TORUS[1]
        steps = jnp.arange(1, REACH + 1, dtype=jnp.int32)
        hit = offsets[:, :, None] == steps
        slot_of = jnp.where(hit.any(axis=1), jnp.argmax(hit, axis=1), SLOTS)
        slot_of = jnp.pad(slot_of.astype(jnp.int32), ((0, REACH), (0, 0)), constant_values=SLOTS)
        vector = pltpu.VMEM((blocks, MODES, WIDTH), jnp.float32)
        extended = pltpu.VMEM((blocks + REACH, MODES, WIDTH), jnp.float32)
        halo = pltpu.VMEM((apps, REACH, MODES, WIDTH), jnp.float32)
        outs = pl.pallas_call(
            lambda *refs: solve_kernel((count, blocks), *refs),
            out_shape=[jax.ShapeDtypeStruct((blocks, WIDTH), jnp.float32)] * 2,
            in_specs=[
                pl.BlockSpec(memory_space=pltpu.VMEM),
                pl.BlockSpec(memory_space=pltpu.VMEM),
                pl.BlockSpec(memory_space=pltpu.SMEM),
                pl.BlockSpec(memory_space=pltpu.SMEM),
                pl.BlockSpec(memory_space=pltpu.VMEM),
                pl.BlockSpec(memory_space=pltpu.VMEM),
            ],
            out_specs=[pl.BlockSpec(memory_space=pltpu.VMEM)] * 2,
            scratch_shapes=[
                pltpu.VMEM((blocks, WIDTH), jnp.float32),
                pltpu.VMEM((blocks + REACH, SLOTS + 1, MODES, WIDTH), jnp.float32),
                extended,
                extended,
                extended,
                extended,
                vector,
                vector,
                vector,
                vector,
                vector,
                halo,
                halo,
                halo,
                pltpu.VMEM((apps, 2, MODES, WIDTH), jnp.float32),
                pltpu.VMEM((apps, MODES, WIDTH), jnp.float32),
                pltpu.VMEM((apps, 2, side, MODES, WIDTH), jnp.float32),
                pltpu.VMEM((apps, 2, MODES, WIDTH), jnp.float32),
                pltpu.SemaphoreType.DMA((apps, 2)),
                pltpu.SemaphoreType.DMA((apps, 2)),
                pltpu.SemaphoreType.DMA((apps, 2)),
                pltpu.SemaphoreType.DMA((apps, 2)),
                pltpu.SemaphoreType.DMA((apps, 2, side)),
                pltpu.SemaphoreType.DMA((apps, 2, side)),
            ],
            compiler_params=pltpu.CompilerParams(
                collective_id=0, has_side_effects=True, vmem_limit_bytes=48 << 20
            ),
            name="lobpcg",
        )(
            diag_blocks,
            coupling,
            offsets,
            slot_of,
            mass.reshape(blocks, WIDTH),
            initial_modes,
        )
        return outs[0].reshape(-1), outs[1].reshape(-1)

    spec = ("sub", "row")
    return jax.shard_map(
        local,
        mesh=mesh,
        in_specs=(
            P(spec, None, None),
            P(spec, None, None, None),
            P(spec, None),
            P(spec),
            P(None, spec),
        ),
        out_specs=(P(spec), P(spec)),
        check_vma=False,
    )
```

time: 1050 us -> 156 us (0.15)
  waiting for transfers between devices: 378 us -> 0 us
  matrix products: 173 us -> 0 us
  loops' own time: 168 us -> 0 us
  Pallas kernels: 0 us -> 146 us
  blocking collectives: 121 us -> 0 us
  other arithmetic: 101 us -> 2.06 us
  starting transfers between devices: 38.4 us -> 0 us
  local copies, waits for them, and re-layouts: 39.7 us -> 6.91 us
  between operations: 22.1 us -> 0.65 us
    psum x6 -> x0, waiting for transfers between devices: 377 us -> none  [one_axis_at_a_time(): value = lax.psum(value, axis)]
    dot_general x233 -> x0, matrix products: 170 us -> none  [the longest x84 69.6 us: purify_step(): cube = jnp.dot(square, density, precision=PRECISE)]
    another operation x3 -> x0, loops' own time: 168 us -> none  [purify(): return lax.fori_loop(0, steps_count, purify_step, initial)]
    pallas_call x0 -> x1, Pallas kernels: none -> 146 us  [local(): pl.pallas_call(lambda *refs: solve_kernel((count, blocks), *refs), out_sh...]
    psum x6 -> x0, blocking collectives: 121 us -> none  [one_axis_at_a_time(): value = lax.psum(value, axis)]
    another operation x40 -> x1, other arithmetic: 82.7 us -> 1.28 us  [local(): slot_of = jnp.where(hit.any(axis=1), jnp.argmax(hit, axis=1), SLOTS)]
    ppermute x8 -> x0, starting transfers between devices: 37.8 us -> none  [from_behind(): lax.ppermute(value, axis, [(source, source + steps) for source in range(i...]
    gather x9 -> x0, local copies, waits for them, and re-layouts: 11.3 us -> none  [the longest x4 4.67 us: ritz_basis(): scaling = lax.rsqrt(jnp.diagonal(gram_mass) + 1e-06)]
  transfers between devices with their start and end apart: 14 -> 0, of which waited for: 6 -> 0; matrix products, arithmetic and copies ran while one was open for 7% -> 0% of each run, Pallas kernels for 0% -> 0%
where the time goes in v1:
time: 156 us
  Pallas kernels  146 us (94%)
  local copies, waits for them, and re-layouts  6.91 us (4%)
  other arithmetic  2.06 us (1%)
    pallas_call x1, Pallas kernels, local(): pl.pallas_call(lambda *refs: solve_kernel((count, blocks), *refs), out_sh...  146 us
    unnamed x11, local copies, waits for them, and re-layouts  6.72 us

profile of v1, /device:TPU:513, one launch (start us, length us, event | category | flops | bytes accessed | tf_op | source)
XLA Modules:
  0.0 155.7 jit_solution(10940019226545220604)
XLA Ops:
  0.6 0.8 compare_reduce_fusion.1
  1.4 0.1 copy.9
  1.5 1.3 compare_reduce_fusion
  2.8 0.1 copy.10
  2.9 0.8 copy.11.refs_2_
  3.6 0.0 copy-start
  3.6 1.9 %copy-done = f32[16,3,128,128]{3,2,1,0:T(8,128)S(1)} copy-done((f32[16,3,128,128]{3,2,1,0:T(8,128)S(1)}, f32[16,3,128,128]{3,2,1,0:T(8,128)}, u32[]{:S(2)}) %copy-start) | copy-done | bytes 3145752
  5.5 0.0 copy-start.1
  5.5 1.2 copy-done.1
  6.8 0.0 copy-start.2
  6.8 0.9 copy-done.2
  7.7 0.0 copy-start.3
  7.7 0.7 copy-done.3
  8.4 146.1 %lobpcg.1 = (f32[16,128]{1,0:T(8,128)S(1)}, f32[16,128]{1,0:T(8,128)S(1)}) custom-call(f32[16,128,128]{2,1,0:T(8,128)S(1)} %copy-done.1, f32[16,3,128,128]{3,2,1,0:T(8,128)S(1)} %copy-done, s32[16,3]{1,0:T(8,128)S(1)} %copy.11.refs_2_, s32[20,4]{1,0:T(8,128)S(1)} %pad.4.refs_3_, f32[16,128]{1,0:T(8,128)S(1)} %bitcast.3, f32[32,2048]{1,0:T(8,128)S(1)} %copy-done.2), custom_call_target="tpu_custom_call" | custom-call | tf_op jit(solution)/shard_map/lobpcg/pallas_call | solution.py:513
  154.5 0.6 copy.14
  155.1 0.6 copy.15
  (3 shorter events, 0.0 us)
Async XLA Ops:
  3.6 1.9 %copy-start = (f32[16,3,128,128]{3,2,1,0:T(8,128)S(1)}, f32[16,3,128,128]{3,2,1,0:T(8,128)}, u32[]{:S(2)}) copy-start(f32[16,3,128,128]{3,2,1,0:T(8,128)} %refs_1_.1) | copy-start | bytes 9437188
  5.5 1.2 copy-start.1
  6.8 0.9 copy-start.2
  7.7 0.7 copy-start.3

commit v2 on v1

v2 whole, which is shorter than its diff:
```python
import jax
import jax.numpy as jnp
from jax import lax
from jax.experimental import pallas as pl
from jax.experimental.pallas import tpu as pltpu
from jax.sharding import PartitionSpec as P

MODES = 32
REACH = 4
SLOTS = 3
ITERS = 3
PURIFY = 28
WIDTH = 128
TORUS = (8, 8, 2)
MESH = pl.DeviceIdType.MESH

HIGH = lax.Precision.HIGH
HIGHEST = lax.Precision.HIGHEST


def mm(a, b, precision):
    return lax.dot_general(
        a, b, (((1,), (0,)), ((), ())), precision=precision, preferred_element_type=jnp.float32
    )


def mm_nt(a, b, precision):
    return lax.dot_general(
        a, b, (((1,), (1,)), ((), ())), precision=precision, preferred_element_type=jnp.float32
    )


def lanes(shape):
    return lax.broadcasted_iota(jnp.int32, shape, 1)


def sublanes(shape):
    return lax.broadcasted_iota(jnp.int32, shape, 0)


def eye(n):
    return (sublanes((n, n)) == lanes((n, n))).astype(jnp.float32)


def total(x):
    return jnp.sum(jnp.sum(x, axis=0, keepdims=True), axis=1, keepdims=True)


def inverse_factor(table, first):
    rows, cols = table.shape
    done = []
    for start in range(0, rows, 8):
        live = table.shape[0]
        column = [
            jnp.broadcast_to(table[:, first + start + k : first + start + k + 1], (live, cols))
            for k in range(8)
        ]
        index = sublanes((live, cols))
        lane = lanes((live, cols))
        for k in range(8):
            at = first + start + k
            pivot = column[k][k : k + 1, :]
            scale = lax.rsqrt(pivot)
            row = jnp.where(lane[0:1] == at, 1.0, table[k : k + 1, :]) * scale
            factor = jnp.where(index > k, column[k] * scale, 0.0)
            table = jnp.where((index > k) & (lane == at), 0.0, table) - factor * row
            table = jnp.where(index == k, row, table)
            for m in range(k + 1, 8):
                column[m] = column[m] - factor * (column[m][k : k + 1, :] * scale)
        done.append(table[:8])
        table = table[8:]
    result = jnp.concatenate(done, axis=0) if len(done) > 1 else done[0]
    shape = (rows, cols)
    return jnp.where(lanes(shape) <= sublanes(shape) + first, result, 0.0)


def purify(matrix):
    n = matrix.shape[0]
    identity = eye(n)
    diagonal = jnp.sum(matrix * identity, axis=0, keepdims=True)
    radius = jnp.sum(jnp.abs(matrix), axis=0, keepdims=True) - jnp.abs(diagonal)
    center = jnp.sum(diagonal, axis=1, keepdims=True) / n
    highest = jnp.max(diagonal + radius, axis=1, keepdims=True)
    lowest = jnp.min(diagonal - radius, axis=1, keepdims=True)
    factor = jnp.minimum(
        MODES / jnp.maximum(highest - center, 1e-6), (n - MODES) / jnp.maximum(center - lowest, 1e-6)
    )
    initial = factor / n * (center * identity - matrix) + MODES / n * identity

    def step(index, density):
        square = mm(density, density, HIGHEST)
        cube = mm(square, density, HIGHEST)
        denominator = total((density - square) * identity)
        numerator = total(square * (identity - density))
        safe = jnp.where(jnp.abs(denominator) > 1e-12, denominator, 1.0)
        ratio = jnp.clip(numerator / safe, 0.0, 1.0)
        up = ratio >= 0.5
        scale = 1.0 / jnp.maximum(jnp.where(up, ratio, 1.0 - ratio), 0.5)
        first = jnp.where(up, 0.0, (1.0 - 2.0 * ratio) * scale)
        second = (1.0 + ratio) * scale
        return first * density + second * square - scale * cube

    return lax.fori_loop(0, PURIFY, step, initial)


def pack(square):
    return jnp.concatenate([square[8 * k : 8 * k + 8] for k in range(4)], axis=1)


def unpack(tile):
    return jnp.concatenate([tile[:, MODES * k : MODES * (k + 1)] for k in range(4)], axis=0)


def scales(gram_mass):
    masked = gram_mass * eye(gram_mass.shape[0])
    across = lax.rsqrt(jnp.sum(masked, axis=0, keepdims=True) + 1e-6)
    down = lax.rsqrt(jnp.sum(masked, axis=1, keepdims=True) + 1e-6)
    return across, gram_mass * down * across


def first_factor(gram_mass):
    across, mass = scales(0.5 * (gram_mass + gram_mass.T))
    return inverse_factor(mass, 0) * across


def next_factor(gram_mass):
    n = gram_mass.shape[0]
    rest = n - MODES
    across, mass = scales(gram_mass)
    lead = 1.0 + 1e-6
    side = mass[:, :MODES]
    side = jnp.where(sublanes((n, MODES)) < MODES, 0.0, side)
    lower = mass[MODES:, :]
    schur = lower - lead * mm_nt(side[MODES:], side, HIGHEST)
    lane = lanes((rest, n))
    bottom = inverse_factor(jnp.where(lane < MODES, -lead * lower, schur), MODES)
    shape = (MODES, n)
    unit = jnp.where(lanes(shape) == sublanes(shape), lead**0.5, 0.0)
    return jnp.concatenate([unit, bottom], axis=0) * across


def ritz_rows(reduced, factor):
    n = reduced.shape[0]
    rows = purify(reduced)[:MODES]
    change = inverse_factor(mm_nt(rows, rows, HIGHEST), 0)
    rows = mm(change, rows, HIGHEST)
    coefficients = mm(rows, factor, HIGHEST)
    padded = jnp.concatenate([rows, jnp.zeros((n - MODES, n), jnp.float32)], axis=0)
    projected = mm_nt(mm(rows, reduced, HIGHEST), padded, HIGHEST)
    return coefficients, projected


def solve_kernel(
    sizes,
    diag_hbm,
    coupling_hbm,
    offsets,
    mass_hbm,
    initial_hbm,
    mass_out,
    energy_out,
    diag,
    coupling,
    mass,
    slot_of,
    inverse_diag,
    product,
    ext0,
    ext1,
    ext2,
    ext3,
    stiff_new,
    modes,
    stiff_modes,
    direction,
    stiff_direction,
    edge,
    landing,
    returned,
    part,
    swapped,
    slots,
    summed,
    late_part,
    late_first,
    late_second,
    load_sem,
    matrix_sem,
    halo_send,
    halo_recv,
    swap_send,
    swap_recv,
    ring_send,
    ring_recv,
    late_send,
    late_recv_first,
    late_recv_second,
):
    count, blocks = sizes
    ny, nx, cores = TORUS
    side = nx
    me = lax.axis_index("row")
    core = me % cores
    x = (me // cores) % nx
    y = me // (cores * nx)
    partner = me + 1 - 2 * core
    exts = (ext0, ext1, ext2, ext3)
    groups = blocks // REACH

    def device(px, py, pcore):
        return {"row": (py * nx + px) * cores + pcore}

    def peer(phase, k, pcore):
        along_x = (1 - core) if phase == 0 else core
        return device((x + k * along_x) % nx, (y + k * (1 - along_x)) % ny, pcore)

    def place(phase):
        along_x = (1 - core) if phase == 0 else core
        return x * along_x + y * (1 - along_x)

    barrier = pltpu.get_barrier_semaphore()
    greeted = [{"row": partner}, {"row": (me + 1) % count}, {"row": (me + count - 1) % count}]
    for k in range(1, side):
        for pcore in range(cores):
            greeted += [device((x + k) % nx, y, pcore), device(x, (y + k) % ny, pcore)]
    for other in greeted:
        pl.semaphore_signal(barrier, inc=1, device_id=other, device_id_type=MESH)

    loads = [
        pltpu.make_async_copy(
            initial_hbm.at[:, pl.ds(b * WIDTH, WIDTH)], ext0.at[b + REACH], load_sem.at[b]
        )
        for b in range(blocks)
    ]
    loads.append(pltpu.make_async_copy(mass_hbm, mass, load_sem.at[blocks]))
    matrix_loads = [
        [
            pltpu.make_async_copy(
                ref.at[pl.ds(g * REACH, REACH)], out.at[pl.ds(g * REACH, REACH)], matrix_sem.at[i, g]
            )
            for i, (ref, out) in enumerate([(diag_hbm, diag), (coupling_hbm, coupling)])
        ]
        for g in range(groups)
    ]
    for copy in loads:
        copy.start()
    for pair in matrix_loads:
        for copy in pair:
            copy.start()

    def send(source, target, send_sem, recv_sem, other):
        return pltpu.make_async_remote_copy(
            src_ref=source,
            dst_ref=target,
            send_sem=send_sem,
            recv_sem=recv_sem,
            device_id=other,
            device_id_type=MESH,
        )

    def forward(app):
        return send(
            exts[app].at[pl.ds(blocks, REACH)],
            landing.at[app],
            halo_send.at[app, 0],
            halo_recv.at[app, 0],
            {"row": me + 1},
        )

    def backward(app):
        return send(
            edge.at[app],
            returned.at[app],
            halo_send.at[app, 1],
            halo_recv.at[app, 1],
            {"row": me - 1},
        )

    def own_products(ext, b):
        weights = jnp.concatenate([diag[b]] + [coupling[b, s] for s in range(SLOTS)], axis=1)
        out = mm(ext[b + REACH], weights, HIGH)
        stiff_new[b] = out[:, :WIDTH]
        for s in range(SLOTS):
            product[b, s] = out[:, (s + 1) * WIDTH : (s + 2) * WIDTH]

    def other_products(ext, b):
        taken = jnp.concatenate([ext[b + REACH - offsets[b, s]] for s in range(SLOTS)], axis=1)
        weights = jnp.concatenate([coupling[b, s] for s in range(SLOTS)], axis=1)
        spread = [product[b + d, slot_of[b + d, d - 1]] for d in range(1, REACH + 1)]
        spread = (spread[0] + spread[1]) + (spread[2] + spread[3])
        stiff_new[b] = stiff_new[b] + mm_nt(taken, weights, HIGH) + spread

    def apply_stiffness(app, ready, hooks):
        ext = exts[app]
        ready(0)
        for b in range(REACH):
            own_products(ext, b)
        for e in range(REACH):
            out = jnp.zeros((MODES, WIDTH), jnp.float32)
            for b in range(e + 1):
                out = out + product[b, slot_of[b, b - e + REACH - 1]]
            edge[app, e] = out
        hooks[0]()

        @pl.when(me < count - 1)
        def _():
            forward(app).start()

        @pl.when(me > 0)
        def _():
            backward(app).start()

        for g in range(1, groups):
            ready(g)
            for b in range(g * REACH, (g + 1) * REACH):
                own_products(ext, b)
        hooks[1]()
        for b in range(REACH, blocks):
            other_products(ext, b)
        hooks[2]()

        @pl.when(me > 0)
        def _():
            forward(app).wait_recv()
            ext[0:REACH] = landing[app]

        @pl.when(me == 0)
        def _():
            ext[0:REACH] = jnp.zeros((REACH, MODES, WIDTH), jnp.float32)

        for b in range(REACH):
            other_products(ext, b)

        @pl.when(me < count - 1)
        def _():
            backward(app).wait_recv()
            for k in range(REACH):
                b = blocks - REACH + k
                stiff_new[b] = stiff_new[b] + returned[app, k]

    def swap(app, stage):
        if stage == 0:
            source, target = part.at[app, 1 - core], swapped.at[app]
        else:
            source, target = summed.at[app, core], summed.at[app, core]
        return send(
            source, target, swap_send.at[app, stage], swap_recv.at[app, stage], {"row": partner}
        )

    def ring(app, phase, k, slot):
        return send(
            slots.at[app, phase, slot],
            slots.at[app, phase, slot],
            ring_send.at[app, phase, k],
            ring_recv.at[app, phase, slot],
            peer(phase, k, core),
        )

    def ring_start(app, phase, value):
        mine = place(phase)
        slots[app, phase, mine] = value
        for k in range(1, side):
            ring(app, phase, k, mine).start()

    def ring_finish(app, phase):
        mine = place(phase)
        for k in range(1, side):
            ring(app, phase, k, (mine + k) % side).wait_recv()
        value = slots[app, phase, 0]
        for k in range(1, side):
            value = value + slots[app, phase, k]
        return value

    def early_first(app):
        swap(app, 0).wait_recv()
        ring_start(app, 0, part[app, core] + swapped[app])

    def early_second(app):
        ring_start(app, 1, ring_finish(app, 0))

    def early_third(app):
        summed[app, core] = ring_finish(app, 1)
        swap(app, 1).start()

    def early_last(app):
        send(
            summed.at[app, core],
            summed.at[app, 1 - core],
            swap_send.at[app, 1],
            swap_recv.at[app, 1],
            {"row": partner},
        ).wait_recv()
        return summed[app, 0], summed[app, 1]

    def late_first_send(app, half, k):
        along_x = 1 - half
        target = device((x + k * along_x) % nx, (y + k * half) % ny, half)
        slot = (x * along_x + y * half) * cores + core
        return send(
            late_part.at[app, half],
            late_first.at[app, slot],
            late_send.at[app, 0, half, k],
            late_recv_first.at[app, slot],
            target,
        )

    def late_first_partner(app):
        half = 1 - core
        slot = (x * core + y * half) * cores + core
        return send(
            late_part.at[app, half],
            late_first.at[app, slot],
            late_send.at[app, 0, half, 0],
            late_recv_first.at[app, slot],
            {"row": partner},
        )

    def late_second_send(app, pcore, k):
        where = place(1)
        return send(
            late_second.at[app, core, where],
            late_second.at[app, core, where],
            late_send.at[app, 1, pcore, k],
            late_recv_second.at[app, core, where],
            peer(1, k, pcore),
        )

    def late_second_partner(app):
        where = place(1)
        return send(
            late_second.at[app, core, where],
            late_second.at[app, core, where],
            late_send.at[app, 1, 1 - core, 0],
            late_recv_second.at[app, core, where],
            {"row": partner},
        )

    def late_start(app, block):
        tile = pack(block)
        late_part[app, 0] = tile[0:4]
        late_part[app, 1] = tile[4:8]
        late_first[app, place(0) * cores + core] = late_part[app, core]
        for k in range(1, side):
            for half in range(2):
                late_first_send(app, half, k).start()
        late_first_partner(app).start()

    def arrived(buffer, sem, index):
        return send(
            buffer.at[index], buffer.at[index], late_send.at[0, 0, 0, 0], sem.at[index], {"row": partner}
        ).wait_recv()

    def late_middle(app):
        mine = place(0) * cores + core
        for k in range(1, side * cores):
            arrived(late_first, late_recv_first, (app, (mine + k) % (side * cores)))
        value = late_first[app, 0]
        for k in range(1, side * cores):
            value = value + late_first[app, k]
        late_second[app, core, place(1)] = value
        for k in range(1, side):
            for pcore in range(cores):
                late_second_send(app, pcore, k).start()
        late_second_partner(app).start()

    def late_finish(app):
        for k in range(1, side):
            arrived(late_second, late_recv_second, (app, core, (place(1) + k) % side))
        for k in range(side):
            arrived(late_second, late_recv_second, (app, 1 - core, k))
        halves = []
        for half in range(2):
            value = late_second[app, half, 0]
            for k in range(1, side):
                value = value + late_second[app, half, k]
            halves.append(value)
        return unpack(jnp.concatenate(halves, axis=0))

    def drain(app):
        @pl.when(me < count - 1)
        def _():
            forward(app).wait_send()

        @pl.when(me > 0)
        def _():
            backward(app).wait_send()

        for stage in range(2):
            swap(app, stage).wait_send()
        for phase in range(2):
            for k in range(1, side):
                ring(app, phase, k, place(phase)).wait_send()
        for k in range(1, side):
            for half in range(2):
                late_first_send(app, half, k).wait_send()
                late_second_send(app, half, k).wait_send()
        late_first_partner(app).wait_send()
        late_second_partner(app).wait_send()

    def wide(refs, group):
        return jnp.concatenate(
            [
                jnp.concatenate([ref[group * REACH + k + shift] for ref, shift in refs], axis=0)
                for k in range(REACH)
            ],
            axis=1,
        )

    def wide_row(ref, group):
        return jnp.concatenate(
            [ref[group * REACH + k : group * REACH + k + 1, :] for k in range(REACH)], axis=1
        )

    def late_block(app):
        ext = exts[app]
        acc = mm_nt(wide([(ext, REACH)], 0), wide([(stiff_new, 0)], 0), HIGH)
        for g in range(1, groups):
            acc = acc + mm_nt(wide([(ext, REACH)], g), wide([(stiff_new, 0)], g), HIGH)
        return acc

    for b in range(blocks):
        for d in range(1, REACH + 1):
            slot = SLOTS
            for s in range(SLOTS):
                slot = jnp.where(offsets[b, s] == d, s, slot)
            slot_of[b, d - 1] = slot
    for b in range(blocks, blocks + REACH):
        for d in range(REACH):
            slot_of[b, d] = SLOTS
    for b in range(blocks + REACH):
        product[b, SLOTS] = jnp.zeros((MODES, WIDTH), jnp.float32)
    part[...] = jnp.zeros(part.shape, jnp.float32)
    for copy in loads:
        copy.wait()
    acc = jnp.zeros((MODES, MODES), jnp.float32)
    for g in range(groups):
        left = wide([(ext0, REACH)], g)
        acc = acc + mm_nt(left * wide_row(mass, g), left, HIGH)
    part[0, 1, :, 0:MODES] = acc

    def ready(g):
        for copy in matrix_loads[g]:
            copy.wait()

    def enter():
        pl.semaphore_wait(barrier, len(greeted))
        swap(0, 0).start()

    apply_stiffness(0, ready, (enter, lambda: early_first(0), lambda: early_second(0)))
    late_start(0, late_block(0))
    identity = eye(WIDTH)
    for b in range(blocks):
        inverse_diag[b : b + 1, :] = 1.0 / jnp.sum(diag[b] * identity, axis=0, keepdims=True)
    late_middle(0)
    early_third(0)
    _, gram_mass = early_last(0)
    factor = first_factor(gram_mass[:, :MODES])
    block = late_finish(0)
    projected = mm_nt(mm(factor, block, HIGHEST), factor, HIGHEST)
    projected = 0.5 * (projected + projected.T)
    coefficients = factor
    basis, stiff_basis = [(ext0, REACH)], [(stiff_new, 0)]
    previous = None

    for step in range(1, ITERS + 1):
        ext = exts[step]
        order = coefficients.shape[1]
        later = jnp.where(lanes((MODES, order)) < MODES, 0.0, coefficients)
        moving = previous is not None
        both = jnp.concatenate([coefficients, later], axis=0) if moving else coefficients
        n = MODES * (3 if moving else 2)
        stiff_acc = jnp.zeros((MODES, n), jnp.float32)
        mass_acc = jnp.zeros((MODES, n), jnp.float32)
        for g in range(groups):
            new = mm(both, wide(basis, g), HIGH)
            stiff = mm(both, wide(stiff_basis, g), HIGH)
            masses = wide_row(mass, g)
            residual = stiff[:MODES] - mm(projected[:, :MODES], new[:MODES] * masses, HIGH)
            residual = residual * wide_row(inverse_diag, g)
            for k in range(REACH):
                b = g * REACH + k
                cut = slice(k * WIDTH, (k + 1) * WIDTH)
                modes[b] = new[:MODES, cut]
                stiff_modes[b] = stiff[:MODES, cut]
                ext[b + REACH] = residual[:, cut]
                if moving:
                    direction[b] = new[MODES:, cut]
                    stiff_direction[b] = stiff[MODES:, cut]
            zero = jnp.zeros(residual.shape, jnp.float32)
            right = [new[:MODES], residual] + ([new[MODES:]] if moving else [])
            stiff_right = [stiff[:MODES], zero] + ([stiff[MODES:]] if moving else [])
            mass_acc = mass_acc + mm_nt(residual * masses, jnp.concatenate(right, axis=0), HIGH)
            stiff_acc = stiff_acc + mm_nt(residual, jnp.concatenate(stiff_right, axis=0), HIGH)
        part[step, 0, :, 0:n] = stiff_acc
        part[step, 1, :, 0:n] = mass_acc
        apply_stiffness(
            step,
            lambda g: None,
            (
                lambda: swap(step, 0).start(),
                lambda: early_first(step),
                lambda: early_second(step),
            ),
        )
        basis = [(modes, 0), (ext, REACH)] + ([(direction, 0)] if moving else [])
        stiff_basis = [(stiff_modes, 0), (stiff_new, 0)] + ([(stiff_direction, 0)] if moving else [])
        late_start(step, late_block(step))
        shape = (MODES, n)
        lane = lanes(shape)
        unit = jnp.where(lane == sublanes(shape), 1.0, 0.0)
        placed = mm(0.5 * projected[:, :MODES], unit, HIGHEST)
        third = []
        if moving:
            zero = jnp.zeros((MODES, order), jnp.float32)
            spread_rows = jnp.concatenate([coefficients, zero, later], axis=0)
            third = [
                [
                    mm_nt(mm(later, old, HIGHEST), spread_rows, HIGHEST)
                    * jnp.where(lane < 2 * MODES, 1.0, 0.5)
                ]
                for old in previous
            ]
        else:
            third = [[], []]
        late_middle(step)
        early_third(step)
        drain(step - 1)
        early_stiff, early_mass = early_last(step)
        half = jnp.where((lane >= MODES) & (lane < 2 * MODES), 0.5, 1.0)
        rest = jnp.concatenate([placed, early_stiff[:, :n]] + third[0], axis=0)
        gram_mass = jnp.concatenate([0.5 * unit, early_mass[:, :n] * half] + third[1], axis=0)
        rest = rest + rest.T
        gram_mass = gram_mass + gram_mass.T
        factor = next_factor(gram_mass)
        known = mm_nt(mm(factor, rest, HIGHEST), factor, HIGHEST)
        middle = factor[:, MODES : 2 * MODES]
        block = late_finish(step)
        reduced = known + mm_nt(mm(middle, block, HIGHEST), middle, HIGHEST)
        reduced = 0.5 * (reduced + reduced.T)
        coefficients, projected = ritz_rows(reduced, factor)
        if step < ITERS:
            spot = jnp.where(lane == sublanes(shape) + MODES, 1.0, 0.0)
            inner = [jnp.zeros(shape, jnp.float32), mm(block, spot, HIGHEST)]
            inner += [jnp.zeros(shape, jnp.float32)] * (n // MODES - 2)
            previous = [rest + jnp.concatenate(inner, axis=0), gram_mass]

    for g in range(groups):
        new = mm(coefficients, wide(basis, g), HIGH)
        stiff = mm(coefficients, wide(stiff_basis, g), HIGH)
        density = jnp.sum(new * new, axis=0, keepdims=True)
        energy = jnp.sum(new * stiff, axis=0, keepdims=True)
        for k in range(REACH):
            cut = slice(k * WIDTH, (k + 1) * WIDTH)
            mass_out[g * REACH + k : g * REACH + k + 1, :] = density[:, cut]
            energy_out[g * REACH + k : g * REACH + k + 1, :] = energy[:, cut]
    drain(ITERS)


def solution(mesh):
    count = mesh.shape["row"]

    def local(diag_blocks, coupling, offsets, mass, initial_modes):
        blocks = diag_blocks.shape[0]
        apps = ITERS + 1
        side = TORUS[1]
        cores = TORUS[2]
        f32 = jnp.float32
        dma = pltpu.SemaphoreType.DMA
        vector = pltpu.VMEM((blocks, MODES, WIDTH), f32)
        extended = pltpu.VMEM((blocks + REACH, MODES, WIDTH), f32)
        halo = pltpu.VMEM((apps, REACH, MODES, WIDTH), f32)
        squares, energies = pl.pallas_call(
            lambda *refs: solve_kernel((count, blocks), *refs),
            out_shape=[jax.ShapeDtypeStruct((blocks, WIDTH), f32)] * 2,
            in_specs=[
                pl.BlockSpec(memory_space=pl.ANY),
                pl.BlockSpec(memory_space=pl.ANY),
                pl.BlockSpec(memory_space=pltpu.SMEM),
                pl.BlockSpec(memory_space=pl.ANY),
                pl.BlockSpec(memory_space=pl.ANY),
            ],
            out_specs=[pl.BlockSpec(memory_space=pltpu.VMEM)] * 2,
            scratch_shapes=[
                pltpu.VMEM((blocks, WIDTH, WIDTH), f32),
                pltpu.VMEM((blocks, SLOTS, WIDTH, WIDTH), f32),
                pltpu.VMEM((blocks, WIDTH), f32),
                pltpu.SMEM((blocks + REACH, REACH), jnp.int32),
                pltpu.VMEM((blocks, WIDTH), f32),
                pltpu.VMEM((blocks + REACH, SLOTS + 1, MODES, WIDTH), f32),
                extended,
                extended,
                extended,
                extended,
                vector,
                vector,
                vector,
                vector,
                vector,
                halo,
                halo,
                halo,
                pltpu.VMEM((apps, 2, MODES, WIDTH), f32),
                pltpu.VMEM((apps, MODES, WIDTH), f32),
                pltpu.VMEM((apps, 2, side, MODES, WIDTH), f32),
                pltpu.VMEM((apps, 2, MODES, WIDTH), f32),
                pltpu.VMEM((apps, 2, 4, WIDTH), f32),
                pltpu.VMEM((apps, side * cores, 4, WIDTH), f32),
                pltpu.VMEM((apps, 2, side, 4, WIDTH), f32),
                dma((blocks + 1,)),
                dma((2, blocks // REACH)),
                dma((apps, 2)),
                dma((apps, 2)),
                dma((apps, 2)),
                dma((apps, 2)),
                dma((apps, 2, side)),
                dma((apps, 2, side)),
                dma((apps, 2, 2, side)),
                dma((apps, side * cores)),
                dma((apps, 2, side)),
            ],
            compiler_params=pltpu.CompilerParams(
                collective_id=0, has_side_effects=True, vmem_limit_bytes=60 << 20
            ),
            name="lobpcg",
        )(diag_blocks, coupling, offsets, mass.reshape(blocks, WIDTH), initial_modes)
        weight = count * blocks * WIDTH / MODES
        return weight * mass * squares.reshape(-1), weight * energies.reshape(-1)

    spec = ("sub", "row")
    return jax.shard_map(
        local,
        mesh=mesh,
        in_specs=(
            P(spec, None, None),
            P(spec, None, None, None),
            P(spec, None),
            P(spec),
            P(None, spec),
        ),
        out_specs=(P(spec), P(spec)),
        check_vma=False,
    )
```

time: 156 us -> 147 us (0.942)
  local copies, waits for them, and re-layouts: 6.91 us -> 1.37 us
  Pallas kernels: 146 us -> 142 us
    unnamed x11 -> x3, local copies, waits for them, and re-layouts: 6.72 us -> 1.37 us
    pallas_call x1, Pallas kernels: 146 us -> 142 us  [local(): pl.pallas_call(lambda *refs: solve_kernel((count, blocks), *refs), out_sh...]
    mul x0 -> x2, other arithmetic: none -> 2.59 us  [local(): return (weight * mass * squares.reshape(-1), weight * energies.reshape(-1))]
where the time goes in v2:
time: 147 us; the launch traced here: 146 us
  Pallas kernels  142 us (97%)
  other arithmetic  2.59 us (2%)
    pallas_call x1, Pallas kernels, local(): pl.pallas_call(lambda *refs: solve_kernel((count, blocks), *refs), out_sh...  142 us

profile of v2, /device:TPU:513, one launch (start us, length us, event | category | flops | bytes accessed | tf_op | source)
XLA Modules:
  0.0 146.2 jit_solution(17678356118464234506)
XLA Ops:
  0.6 0.0 copy-start
  0.6 1.4 copy.7.refs_2_
  2.0 141.6 %lobpcg.1 = (f32[16,128]{1,0:T(8,128)}, f32[16,128]{1,0:T(8,128)}) custom-call(f32[16,128,128]{2,1,0:T(8,128)} %refs_0_.1, f32[16,3,128,128]{3,2,1,0:T(8,128)} %refs_1_.1, s32[16,3]{1,0:T(8,128)} %copy.7.refs_2_, f32[16,128]{1,0:T(8,128)} %bitcast.5, f32[32,2048]{1,0:T(8,128)} %refs_4_.1), custom_call_target="tpu_custom_call" | custom-call | tf_op jit(solution)/shard_map/lobpcg/pallas_call | solution.py:672
  143.6 0.0 copy-done
  143.6 1.3 bitcast_multiply_fusion
  144.9 1.3 multiply_bitcast_fusion
Async XLA Ops:
  0.6 143.0 %copy-start = (f32[2048]{0:T(1024)S(1)}, f32[2048]{0:T(1024)}, u32[]{:S(2)}) copy-start(f32[2048]{0:T(1024)} %param.8) | copy-start | bytes 24580

commit v3 on v2

v3 whole, which is shorter than its diff:
```python
import jax
import jax.numpy as jnp
from jax import lax
from jax.experimental import pallas as pl
from jax.experimental.pallas import tpu as pltpu
from jax.sharding import PartitionSpec as P

MODES = 32
REACH = 4
SLOTS = 3
ITERS = 3
PURIFY = 28
WIDTH = 128
TORUS = (8, 8, 2)
MESH = pl.DeviceIdType.MESH
CHANNELS = ((1, 1), (2, 1, 1), (3, 2, 1), (3, 2, 1))

HIGHEST = lax.Precision.HIGHEST


def mm(a, b, precision):
    return lax.dot_general(
        a, b, (((1,), (0,)), ((), ())), precision=precision, preferred_element_type=jnp.float32
    )


def mm_nt(a, b, precision):
    return lax.dot_general(
        a, b, (((1,), (1,)), ((), ())), precision=precision, preferred_element_type=jnp.float32
    )


def split(value):
    high = value.astype(jnp.bfloat16)
    return high, (value - high.astype(jnp.float32)).astype(jnp.bfloat16)


def mm3(a, b, transposed=False):
    contract = (((1,), (1 if transposed else 0,)), ((), ()))
    a_high, a_low = split(a)
    b_high, b_low = b if isinstance(b, tuple) else split(b)
    rows = a.shape[0]
    top = lax.dot_general(
        jnp.concatenate([a_high, a_low], axis=0),
        b_high,
        contract,
        preferred_element_type=jnp.float32,
    )
    rest = lax.dot_general(a_high, b_low, contract, preferred_element_type=jnp.float32)
    return (top[:rows] + rest) + top[rows:]


def lanes(shape):
    return lax.broadcasted_iota(jnp.int32, shape, 1)


def sublanes(shape):
    return lax.broadcasted_iota(jnp.int32, shape, 0)


def eye(n):
    return (sublanes((n, n)) == lanes((n, n))).astype(jnp.float32)


def total(x):
    return jnp.sum(jnp.sum(x, axis=0, keepdims=True), axis=1, keepdims=True)


def inverse_factor(table, first):
    rows, cols = table.shape
    done = []
    for start in range(0, rows, 8):
        live = table.shape[0]
        column = [
            jnp.broadcast_to(table[:, first + start + k : first + start + k + 1], (live, cols))
            for k in range(8)
        ]
        index = sublanes((live, cols))
        lane = lanes((live, cols))
        for k in range(8):
            at = first + start + k
            pivot = column[k][k : k + 1, :]
            scale = lax.rsqrt(pivot)
            row = jnp.where(lane[0:1] == at, 1.0, table[k : k + 1, :]) * scale
            factor = jnp.where(index > k, column[k] * scale, 0.0)
            table = jnp.where((index > k) & (lane == at), 0.0, table) - factor * row
            table = jnp.where(index == k, row, table)
            for m in range(k + 1, 8):
                column[m] = column[m] - factor * (column[m][k : k + 1, :] * scale)
        done.append(table[:8])
        table = table[8:]
    result = jnp.concatenate(done, axis=0) if len(done) > 1 else done[0]
    shape = (rows, cols)
    return jnp.where(lanes(shape) <= sublanes(shape) + first, result, 0.0)


def purify(matrix):
    n = matrix.shape[0]
    identity = eye(n)
    diagonal = jnp.sum(matrix * identity, axis=0, keepdims=True)
    radius = jnp.sum(jnp.abs(matrix), axis=0, keepdims=True) - jnp.abs(diagonal)
    center = jnp.sum(diagonal, axis=1, keepdims=True) / n
    highest = jnp.max(diagonal + radius, axis=1, keepdims=True)
    lowest = jnp.min(diagonal - radius, axis=1, keepdims=True)
    factor = jnp.minimum(
        MODES / jnp.maximum(highest - center, 1e-6), (n - MODES) / jnp.maximum(center - lowest, 1e-6)
    )
    initial = factor / n * (center * identity - matrix) + MODES / n * identity

    def step(index, density):
        square = mm(density, density, HIGHEST)
        cube = mm(square, density, HIGHEST)
        denominator = total((density - square) * identity)
        numerator = total(square * (identity - density))
        safe = jnp.where(jnp.abs(denominator) > 1e-12, denominator, 1.0)
        ratio = jnp.clip(numerator / safe, 0.0, 1.0)
        up = ratio >= 0.5
        scale = 1.0 / jnp.maximum(jnp.where(up, ratio, 1.0 - ratio), 0.5)
        first = jnp.where(up, 0.0, (1.0 - 2.0 * ratio) * scale)
        second = (1.0 + ratio) * scale
        return first * density + second * square - scale * cube

    return lax.fori_loop(0, PURIFY, step, initial)


def pack32(block):
    return jnp.concatenate([block[8 * k : 8 * k + 8] for k in range(4)], axis=1)


def unpack32(tile):
    return jnp.concatenate([tile[:, MODES * k : MODES * (k + 1)] for k in range(4)], axis=0)


def pack64(block):
    return jnp.concatenate([block[:16], block[16:]], axis=1)


def unpack64(tile):
    return jnp.concatenate([tile[:, : 2 * MODES], tile[:, 2 * MODES :]], axis=0)


def pack96(block):
    last = [block[24:, MODES * k : MODES * (k + 1)] for k in range(3)]
    return jnp.concatenate([block[:24], jnp.concatenate(last, axis=0)], axis=1)


def unpack96(tile):
    last = [tile[8 * k : 8 * k + 8, 3 * MODES :] for k in range(3)]
    return jnp.concatenate([tile[:, : 3 * MODES], jnp.concatenate(last, axis=1)], axis=0)


def scales(gram_mass):
    masked = gram_mass * eye(gram_mass.shape[0])
    across = lax.rsqrt(jnp.sum(masked, axis=0, keepdims=True) + 1e-6)
    down = lax.rsqrt(jnp.sum(masked, axis=1, keepdims=True) + 1e-6)
    return across, gram_mass * down * across


def first_factor(gram_mass):
    across, mass = scales(0.5 * (gram_mass + gram_mass.T))
    return inverse_factor(mass, 0) * across


def next_factor(gram_mass):
    n = gram_mass.shape[0]
    rest = n - MODES
    across, mass = scales(gram_mass)
    lead = 1.0 + 1e-6
    side = mass[:, :MODES]
    side = jnp.where(sublanes((n, MODES)) < MODES, 0.0, side)
    lower = mass[MODES:, :]
    schur = lower - lead * mm_nt(side[MODES:], side, HIGHEST)
    lane = lanes((rest, n))
    bottom = inverse_factor(jnp.where(lane < MODES, -lead * lower, schur), MODES)
    shape = (MODES, n)
    unit = jnp.where(lanes(shape) == sublanes(shape), lead**0.5, 0.0)
    return jnp.concatenate([unit, bottom], axis=0) * across


def ritz_rows(reduced, factor):
    n = reduced.shape[0]
    rows = purify(reduced)[:MODES]
    change = inverse_factor(mm_nt(rows, rows, HIGHEST), 0)
    rows = mm(change, rows, HIGHEST)
    coefficients = mm(rows, factor, HIGHEST)
    padded = jnp.concatenate([rows, jnp.zeros((n - MODES, n), jnp.float32)], axis=0)
    projected = mm_nt(mm(rows, reduced, HIGHEST), padded, HIGHEST)
    return coefficients, projected


def solve_kernel(
    sizes,
    diag_hbm,
    coupling_hbm,
    offsets_hbm,
    mass_hbm,
    initial_hbm,
    mass_out,
    energy_out,
    diag,
    coupling,
    high,
    low,
    mass,
    offsets,
    slot_of,
    inverse_diag,
    product,
    ext0,
    ext1,
    ext2,
    ext3,
    stiff_new,
    modes,
    stiff_modes,
    direction,
    stiff_direction,
    edge,
    landing,
    returned,
    load_sem,
    matrix_sem,
    halo_send,
    halo_recv,
    *channel_refs,
):
    count, blocks = sizes
    ny, nx, cores = TORUS
    side = nx
    me = lax.axis_index("row")
    core = lax.rem(me, cores)
    x = lax.rem(lax.div(me, cores), nx)
    y = lax.div(me, cores * nx)
    partner = me + 1 - 2 * core
    exts = (ext0, ext1, ext2, ext3)
    groups = blocks // REACH

    table_load = pltpu.make_async_copy(offsets_hbm, offsets, load_sem.at[blocks + 1])
    loads = [pltpu.make_async_copy(mass_hbm, mass, load_sem.at[blocks])]
    loads += [
        pltpu.make_async_copy(
            initial_hbm.at[:, pl.ds(b * WIDTH, WIDTH)], ext0.at[b + REACH], load_sem.at[b]
        )
        for b in range(blocks)
    ]
    matrix_loads = [
        [
            pltpu.make_async_copy(
                ref.at[pl.ds(g * REACH, REACH)], out.at[pl.ds(g * REACH, REACH)], matrix_sem.at[i, g]
            )
            for i, (ref, out) in enumerate([(diag_hbm, diag), (coupling_hbm, coupling)])
        ]
        for g in range(groups)
    ]
    table_load.start()
    for copy in loads:
        copy.start()
    for pair in matrix_loads:
        for copy in pair:
            copy.start()

    x_at = [lax.rem(x + k, nx) for k in range(side)]
    y_at = [lax.rem(y + k, ny) for k in range(side)]

    def device(px, py, pcore):
        return {"row": (py * nx + px) * cores + pcore}

    barrier = pltpu.get_barrier_semaphore()
    greeted = [{"row": partner}, {"row": lax.rem(me + 1, count)}, {"row": lax.rem(me + count - 1, count)}]
    for k in range(1, side):
        for pcore in range(cores):
            greeted += [device(x_at[k], y, pcore), device(x, y_at[k], pcore)]
    for other in greeted:
        pl.semaphore_signal(barrier, inc=1, device_id=other, device_id_type=MESH)

    def send(source, target, send_sem, recv_sem, other):
        return pltpu.make_async_remote_copy(
            src_ref=source,
            dst_ref=target,
            send_sem=send_sem,
            recv_sem=recv_sem,
            device_id=other,
            device_id_type=MESH,
        )

    def forward(app):
        return send(
            exts[app].at[pl.ds(blocks, REACH)],
            landing.at[app],
            halo_send.at[app, 0],
            halo_recv.at[app, 0],
            {"row": me + 1},
        )

    def backward(app):
        return send(
            edge.at[app],
            returned.at[app],
            halo_send.at[app, 1],
            halo_recv.at[app, 1],
            {"row": me - 1},
        )

    def own_products(ext, b):
        out = mm3(ext[b + REACH], (high[b], low[b]))
        stiff_new[b] = out[:, :WIDTH]
        for s in range(SLOTS):
            product[b, s] = out[:, (s + 1) * WIDTH : (s + 2) * WIDTH]

    def other_products(ext, b):
        taken = jnp.concatenate([ext[b + REACH - offsets[b, s]] for s in range(SLOTS)], axis=1)
        spread = [product[b + d, slot_of[b + d, d - 1]] for d in range(1, REACH + 1)]
        spread = (spread[0] + spread[1]) + (spread[2] + spread[3])
        out = mm3(taken, (high[b, :, WIDTH:], low[b, :, WIDTH:]), True)
        stiff_new[b] = stiff_new[b] + out + spread

    def apply_stiffness(app, ready, hooks):
        ext = exts[app]
        ready(0)
        for b in range(REACH):
            own_products(ext, b)
        for e in range(REACH):
            out = jnp.zeros((MODES, WIDTH), jnp.float32)
            for b in range(e + 1):
                out = out + product[b, slot_of[b, b - e + REACH - 1]]
            edge[app, e] = out
        hooks[0]()

        @pl.when(me < count - 1)
        def _():
            forward(app).start()

        @pl.when(me > 0)
        def _():
            backward(app).start()

        for g in range(1, groups):
            ready(g)
            for b in range(g * REACH, (g + 1) * REACH):
                own_products(ext, b)
        hooks[1]()
        for b in range(REACH, blocks):
            other_products(ext, b)

        @pl.when(me > 0)
        def _():
            forward(app).wait_recv()
            ext[0:REACH] = landing[app]

        @pl.when(me == 0)
        def _():
            ext[0:REACH] = jnp.zeros((REACH, MODES, WIDTH), jnp.float32)

        for b in range(REACH):
            other_products(ext, b)

        @pl.when(me < count - 1)
        def _():
            backward(app).wait_recv()
            for k in range(REACH):
                b = blocks - REACH + k
                stiff_new[b] = stiff_new[b] + returned[app, k]

    class Channel:
        def __init__(self, refs):
            (self.part, self.first, self.second, self.sends, self.first_sem, self.second_sem) = refs
            self.own_first = (x * (1 - core) + y * core) * cores + core
            self.own_second = y * (1 - core) + x * core

        def first_send(self, half, k):
            if half == 0:
                slot, target = x * cores + core, device(x_at[k], y, 0)
            else:
                slot, target = y * cores + core, device(x, y_at[k], 1)
            return send(
                self.part.at[half],
                self.first.at[slot],
                self.sends.at[0, half, k],
                self.first_sem.at[slot],
                target,
            )

        def first_partner(self):
            half = 1 - core
            slot = (x * core + y * half) * cores + core
            return send(
                self.part.at[half],
                self.first.at[slot],
                self.sends.at[0, half, 0],
                self.first_sem.at[slot],
                {"row": partner},
            )

        def second_send(self, pcore, k):
            where = self.own_second
            px = x * (1 - core) + x_at[k] * core
            py = y_at[k] * (1 - core) + y * core
            return send(
                self.second.at[core, where],
                self.second.at[core, where],
                self.sends.at[1, pcore, k],
                self.second_sem.at[core, where],
                device(px, py, pcore),
            )

        def second_partner(self):
            where = self.own_second
            return send(
                self.second.at[core, where],
                self.second.at[core, where],
                self.sends.at[1, 1 - core, 0],
                self.second_sem.at[core, where],
                {"row": partner},
            )

        def arrived(self, buffer, sem, index):
            send(
                buffer.at[index], buffer.at[index], self.sends.at[0, 0, 0], sem.at[index],
                {"row": partner},
            ).wait_recv()

        def store(self, packed):
            rows = packed.shape[0] // 2
            self.part[0] = packed[:rows]
            self.part[1] = packed[rows:]

        def start(self):
            self.first[self.own_first] = self.part[core]
            for k in range(1, side):
                for half in range(2):
                    self.first_send(half, k).start()
            self.first_partner().start()

        def middle(self):
            slots = side * cores
            for k in range(1, slots):
                self.arrived(self.first, self.first_sem, lax.rem(self.own_first + k, slots))
            values = [self.first[k] for k in range(slots)]
            while len(values) > 1:
                values = [p + q for p, q in zip(values[::2], values[1::2])]
            self.second[core, self.own_second] = values[0]
            for k in range(1, side):
                for pcore in range(cores):
                    self.second_send(pcore, k).start()
            self.second_partner().start()

        def finish(self):
            for k in range(1, side):
                self.arrived(
                    self.second, self.second_sem, (core, lax.rem(self.own_second + k, side))
                )
            for k in range(side):
                self.arrived(self.second, self.second_sem, (1 - core, k))
            halves = []
            for half in range(2):
                values = [self.second[half, k] for k in range(side)]
                while len(values) > 1:
                    values = [p + q for p, q in zip(values[::2], values[1::2])]
                halves.append(values[0])
            return jnp.concatenate(halves, axis=0)

        def drain(self):
            for k in range(1, side):
                for half in range(2):
                    self.first_send(half, k).wait_send()
                    self.second_send(half, k).wait_send()
            self.first_partner().wait_send()
            self.second_partner().wait_send()

    channels, taken = [], 0
    for tiles in CHANNELS:
        channels.append([])
        for _ in tiles:
            channels[-1].append(Channel(channel_refs[taken : taken + 6]))
            taken += 6

    def drain(app):
        @pl.when(me < count - 1)
        def _():
            forward(app).wait_send()

        @pl.when(me > 0)
        def _():
            backward(app).wait_send()

        for channel in channels[app]:
            channel.drain()

    def wide(refs, group):
        return jnp.concatenate(
            [
                jnp.concatenate([ref[group * REACH + k + shift] for ref, shift in refs], axis=0)
                for k in range(REACH)
            ],
            axis=1,
        )

    def wide_row(ref, group):
        return jnp.concatenate(
            [ref[group * REACH + k : group * REACH + k + 1, :] for k in range(REACH)], axis=1
        )

    def late_block(app):
        ext = exts[app]
        acc = mm3(wide([(ext, REACH)], 0), wide([(stiff_new, 0)], 0), True)
        for g in range(1, groups):
            acc = acc + mm3(wide([(ext, REACH)], g), wide([(stiff_new, 0)], g), True)
        return acc

    for b in range(blocks + REACH):
        product[b, SLOTS] = jnp.zeros((MODES, WIDTH), jnp.float32)
    for copy in loads:
        copy.wait()
    acc = jnp.zeros((MODES, MODES), jnp.float32)
    for g in range(groups):
        left = wide([(ext0, REACH)], g)
        acc = acc + mm3(left * wide_row(mass, g), left, True)
    channels[0][0].store(pack32(acc))
    table_load.wait()
    for b in range(blocks):
        for d in range(1, REACH + 1):
            slot = SLOTS
            for s in range(SLOTS):
                slot = jnp.where(offsets[b, s] == d, s, slot)
            slot_of[b, d - 1] = slot
    for b in range(blocks, blocks + REACH):
        for d in range(REACH):
            slot_of[b, d] = SLOTS

    def ready(g):
        for copy in matrix_loads[g]:
            copy.wait()
        for b in range(g * REACH, (g + 1) * REACH):
            whole = jnp.concatenate([diag[b]] + [coupling[b, s] for s in range(SLOTS)], axis=1)
            high[b], low[b] = split(whole)

    def enter():
        pl.semaphore_wait(barrier, len(greeted))
        channels[0][0].start()

    apply_stiffness(0, ready, (enter, lambda: None))
    channels[0][1].store(pack32(late_block(0)))
    channels[0][1].start()
    identity = eye(WIDTH)
    for b in range(blocks):
        inverse_diag[b : b + 1, :] = 1.0 / jnp.sum(diag[b] * identity, axis=0, keepdims=True)
    channels[0][0].middle()
    channels[0][1].middle()
    factor = first_factor(unpack32(channels[0][0].finish()))
    block = unpack32(channels[0][1].finish())
    projected = mm_nt(mm(factor, block, HIGHEST), factor, HIGHEST)
    projected = 0.5 * (projected + projected.T)
    coefficients = factor
    basis, stiff_basis = [(ext0, REACH)], [(stiff_new, 0)]
    previous = None

    for step in range(1, ITERS + 1):
        ext = exts[step]
        order = coefficients.shape[1]
        later = jnp.where(lanes((MODES, order)) < MODES, 0.0, coefficients)
        moving = previous is not None
        both = jnp.concatenate([coefficients, later], axis=0) if moving else coefficients
        n = MODES * (3 if moving else 2)
        stiff_acc = jnp.zeros((MODES, n - MODES), jnp.float32)
        mass_acc = jnp.zeros((MODES, n), jnp.float32)
        for g in range(groups):
            new = mm3(both, wide(basis, g))
            stiff = mm3(both, wide(stiff_basis, g))
            masses = wide_row(mass, g)
            residual = stiff[:MODES] - mm3(projected[:, :MODES], new[:MODES] * masses)
            residual = residual * wide_row(inverse_diag, g)
            for k in range(REACH):
                b = g * REACH + k
                cut = slice(k * WIDTH, (k + 1) * WIDTH)
                modes[b] = new[:MODES, cut]
                stiff_modes[b] = stiff[:MODES, cut]
                ext[b + REACH] = residual[:, cut]
                if moving:
                    direction[b] = new[MODES:, cut]
                    stiff_direction[b] = stiff[MODES:, cut]
            right = [new[:MODES], residual] + ([new[MODES:]] if moving else [])
            mass_acc = mass_acc + mm3(residual * masses, jnp.concatenate(right, axis=0), True)
            stiff_acc = stiff_acc + mm3(residual, stiff, True)
        mass_sum, stiff_sum, late_sum = channels[step]
        mass_sum.store(pack96(mass_acc) if moving else pack64(mass_acc))
        stiff_sum.store(pack64(stiff_acc) if moving else pack32(stiff_acc))

        def leave(mass_sum=mass_sum, stiff_sum=stiff_sum):
            mass_sum.start()
            stiff_sum.start()

        apply_stiffness(step, lambda g: None, (leave, lambda: None))
        basis = [(modes, 0), (ext, REACH)] + ([(direction, 0)] if moving else [])
        stiff_basis = [(stiff_modes, 0), (stiff_new, 0)] + ([(stiff_direction, 0)] if moving else [])
        late_sum.store(pack32(late_block(step)))
        late_sum.start()
        shape = (MODES, n)
        lane = lanes(shape)
        unit = jnp.where(lane == sublanes(shape), 1.0, 0.0)
        placed = mm(0.5 * projected[:, :MODES], unit, HIGHEST)
        third = []
        if moving:
            zero = jnp.zeros((MODES, order), jnp.float32)
            spread_rows = jnp.concatenate([coefficients, zero, later], axis=0)
            third = [
                [
                    mm_nt(mm(later, old, HIGHEST), spread_rows, HIGHEST)
                    * jnp.where(lane < 2 * MODES, 1.0, 0.5)
                ]
                for old in previous
            ]
        else:
            third = [[], []]
        drain(step - 1)
        mass_sum.middle()
        stiff_sum.middle()
        late_sum.middle()
        early_mass = mass_sum.finish()
        early_mass = unpack96(early_mass) if moving else unpack64(early_mass)
        half = jnp.where((lane >= MODES) & (lane < 2 * MODES), 0.5, 1.0)
        gram_mass = jnp.concatenate([0.5 * unit, early_mass * half] + third[1], axis=0)
        gram_mass = gram_mass + gram_mass.T
        factor = next_factor(gram_mass)
        middle = factor[:, MODES : 2 * MODES]
        early_stiff = stiff_sum.finish()
        early_stiff = unpack64(early_stiff) if moving else unpack32(early_stiff)
        empty = jnp.zeros((MODES, MODES), jnp.float32)
        pieces = [early_stiff[:, :MODES], empty] + ([early_stiff[:, MODES:]] if moving else [])
        rest = jnp.concatenate([placed, jnp.concatenate(pieces, axis=1)] + third[0], axis=0)
        rest = rest + rest.T
        known = mm_nt(mm(factor, rest, HIGHEST), factor, HIGHEST)
        block = unpack32(late_sum.finish())
        reduced = known + mm_nt(mm(middle, block, HIGHEST), middle, HIGHEST)
        reduced = 0.5 * (reduced + reduced.T)
        coefficients, projected = ritz_rows(reduced, factor)
        if step < ITERS:
            spot = jnp.where(lane == sublanes(shape) + MODES, 1.0, 0.0)
            inner = [jnp.zeros(shape, jnp.float32), mm(block, spot, HIGHEST)]
            inner += [jnp.zeros(shape, jnp.float32)] * (n // MODES - 2)
            previous = [rest + jnp.concatenate(inner, axis=0), gram_mass]

    weight = count * blocks * WIDTH / MODES
    for g in range(groups):
        new = mm3(coefficients, wide(basis, g))
        stiff = mm3(coefficients, wide(stiff_basis, g))
        density = weight * wide_row(mass, g) * jnp.sum(new * new, axis=0, keepdims=True)
        energy = weight * jnp.sum(new * stiff, axis=0, keepdims=True)
        for k in range(REACH):
            cut = slice(k * WIDTH, (k + 1) * WIDTH)
            mass_out[g * REACH + k : g * REACH + k + 1, :] = density[:, cut]
            energy_out[g * REACH + k : g * REACH + k + 1, :] = energy[:, cut]
    drain(ITERS)


def solution(mesh):
    count = mesh.shape["row"]

    def local(diag_blocks, coupling, offsets, mass, initial_modes):
        blocks = diag_blocks.shape[0]
        apps = ITERS + 1
        side = TORUS[1]
        cores = TORUS[2]
        f32 = jnp.float32
        dma = pltpu.SemaphoreType.DMA
        vector = pltpu.VMEM((blocks, MODES, WIDTH), f32)
        extended = pltpu.VMEM((blocks + REACH, MODES, WIDTH), f32)
        halo = pltpu.VMEM((apps, REACH, MODES, WIDTH), f32)
        channel_shapes = []
        for tiles in CHANNELS:
            for tile in tiles:
                rows = 4 * tile
                channel_shapes += [
                    pltpu.VMEM((2, rows, WIDTH), f32),
                    pltpu.VMEM((side * cores, rows, WIDTH), f32),
                    pltpu.VMEM((2, side, rows, WIDTH), f32),
                    dma((2, 2, side)),
                    dma((side * cores,)),
                    dma((2, side)),
                ]
        outs = pl.pallas_call(
            lambda *refs: solve_kernel((count, blocks), *refs),
            out_shape=[jax.ShapeDtypeStruct((blocks, WIDTH), f32)] * 2,
            in_specs=[
                pl.BlockSpec(memory_space=pl.ANY),
                pl.BlockSpec(memory_space=pl.ANY),
                pl.BlockSpec(memory_space=pl.ANY),
                pl.BlockSpec(memory_space=pl.ANY),
                pl.BlockSpec(memory_space=pl.ANY),
            ],
            out_specs=[pl.BlockSpec(memory_space=pltpu.VMEM)] * 2,
            scratch_shapes=[
                pltpu.VMEM((blocks, WIDTH, WIDTH), f32),
                pltpu.VMEM((blocks, SLOTS, WIDTH, WIDTH), f32),
                pltpu.VMEM((blocks, WIDTH, (SLOTS + 1) * WIDTH), jnp.bfloat16),
                pltpu.VMEM((blocks, WIDTH, (SLOTS + 1) * WIDTH), jnp.bfloat16),
                pltpu.VMEM((blocks, WIDTH), f32),
                pltpu.SMEM((blocks, SLOTS), jnp.int32),
                pltpu.SMEM((blocks + REACH, REACH), jnp.int32),
                pltpu.VMEM((blocks, WIDTH), f32),
                pltpu.VMEM((blocks + REACH, SLOTS + 1, MODES, WIDTH), f32),
                extended,
                extended,
                extended,
                extended,
                vector,
                vector,
                vector,
                vector,
                vector,
                halo,
                halo,
                halo,
                dma((blocks + 2,)),
                dma((2, blocks // REACH)),
                dma((apps, 2)),
                dma((apps, 2)),
                *channel_shapes,
            ],
            compiler_params=pltpu.CompilerParams(
                collective_id=0, has_side_effects=True, vmem_limit_bytes=60 << 20
            ),
            name="lobpcg",
        )(diag_blocks, coupling, offsets, mass.reshape(blocks, WIDTH), initial_modes)
        return outs[0].reshape(-1), outs[1].reshape(-1)

    spec = ("sub", "row")
    return jax.shard_map(
        local,
        mesh=mesh,
        in_specs=(
            P(spec, None, None),
            P(spec, None, None, None),
            P(spec, None),
            P(spec),
            P(None, spec),
        ),
        out_specs=(P(spec), P(spec)),
        check_vma=False,
    )
```

time: 147 us -> 138 us (0.939)
  Pallas kernels: 142 us -> 133 us
  other arithmetic: 2.59 us -> 0 us
  local copies, waits for them, and re-layouts: 1.37 us -> 3.95 us
    pallas_call x1, Pallas kernels: 142 us -> 133 us  [local(): pl.pallas_call(lambda *refs: solve_kernel((count, blocks), *refs), out_sh...]
    mul x2 -> x0, other arithmetic: 2.59 us -> none  [local(): return (weight * mass * squares.reshape(-1), weight * energies.reshape(-1))]
    unnamed x3, local copies, waits for them, and re-layouts: 1.37 us -> 3.95 us
where the time goes in v3:
time: 138 us
  Pallas kernels  133 us (96%)
  local copies, waits for them, and re-layouts  3.95 us (3%)
    pallas_call x1, Pallas kernels, local(): pl.pallas_call(lambda *refs: solve_kernel((count, blocks), *refs), out_sh...  133 us
    unnamed x3, local copies, waits for them, and re-layouts  3.95 us

profile of v3, /device:TPU:513, one launch (start us, length us, event | category | flops | bytes accessed | tf_op | source)
XLA Modules:
  0.0 137.9 jit_solution(12189119062024740062)
XLA Ops:
  0.6 1.4 copy.7.refs_2_
  2.0 133.3 %lobpcg.1 = (f32[16,128]{1,0:T(8,128)}, f32[16,128]{1,0:T(8,128)}) custom-call(f32[16,128,128]{2,1,0:T(8,128)} %refs_0_.1, f32[16,3,128,128]{3,2,1,0:T(8,128)} %refs_1_.1, s32[16,3]{1,0:T(8,128)} %copy.7.refs_2_, f32[16,128]{1,0:T(8,128)} %bitcast.3, f32[32,2048]{1,0:T(8,128)} %refs_4_.1), custom_call_target="tpu_custom_call" | custom-call | tf_op jit(solution)/shard_map/lobpcg/pallas_call | solution.py:680
  135.3 1.3 copy.10
  136.6 1.3 copy.11

commit v4 on v3

--- a/solution.py
+++ b/solution.py
@@ -108,8 +108,8 @@
     initial = factor / n * (center * identity - matrix) + MODES / n * identity
 
     def step(index, density):
-        square = mm(density, density, HIGHEST)
-        cube = mm(square, density, HIGHEST)
+        square = mm3(density, density)
+        cube = mm3(square, density)
         denominator = total((density - square) * identity)
         numerator = total(square * (identity - density))
         safe = jnp.where(jnp.abs(denominator) > 1e-12, denominator, 1.0)
@@ -149,42 +149,30 @@
     return jnp.concatenate([tile[:, : 3 * MODES], jnp.concatenate(last, axis=1)], axis=0)
 
 
-def scales(gram_mass):
-    masked = gram_mass * eye(gram_mass.shape[0])
-    across = lax.rsqrt(jnp.sum(masked, axis=0, keepdims=True) + 1e-6)
-    down = lax.rsqrt(jnp.sum(masked, axis=1, keepdims=True) + 1e-6)
-    return across, gram_mass * down * across
-
-
 def first_factor(gram_mass):
-    across, mass = scales(0.5 * (gram_mass + gram_mass.T))
-    return inverse_factor(mass, 0) * across
+    return inverse_factor(0.5 * (gram_mass + gram_mass.T), 0)
 
 
 def next_factor(gram_mass):
     n = gram_mass.shape[0]
     rest = n - MODES
-    across, mass = scales(gram_mass)
-    lead = 1.0 + 1e-6
-    side = mass[:, :MODES]
+    side = gram_mass[:, :MODES]
     side = jnp.where(sublanes((n, MODES)) < MODES, 0.0, side)
-    lower = mass[MODES:, :]
-    schur = lower - lead * mm_nt(side[MODES:], side, HIGHEST)
-    lane = lanes((rest, n))
-    bottom = inverse_factor(jnp.where(lane < MODES, -lead * lower, schur), MODES)
+    lower = gram_mass[MODES:, :]
+    schur = lower - mm_nt(side[MODES:], side, HIGHEST)
+    bottom = inverse_factor(jnp.where(lanes((rest, n)) < MODES, -lower, schur), MODES)
     shape = (MODES, n)
-    unit = jnp.where(lanes(shape) == sublanes(shape), lead**0.5, 0.0)
-    return jnp.concatenate([unit, bottom], axis=0) * across
+    unit = jnp.where(lanes(shape) == sublanes(shape), 1.0, 0.0)
+    return jnp.concatenate([unit, bottom], axis=0)
 
 
 def ritz_rows(reduced, factor):
-    n = reduced.shape[0]
     rows = purify(reduced)[:MODES]
     change = inverse_factor(mm_nt(rows, rows, HIGHEST), 0)
-    rows = mm(change, rows, HIGHEST)
     coefficients = mm(rows, factor, HIGHEST)
-    padded = jnp.concatenate([rows, jnp.zeros((n - MODES, n), jnp.float32)], axis=0)
-    projected = mm_nt(mm(rows, reduced, HIGHEST), padded, HIGHEST)
+    projected = mm_nt(mm(rows, reduced, HIGHEST), rows, HIGHEST)
+    coefficients = mm(change, coefficients, HIGHEST)
+    projected = mm_nt(mm(change, projected, HIGHEST), change, HIGHEST)
     return coefficients, projected
 
 
@@ -308,39 +296,42 @@
             product[b, s] = out[:, (s + 1) * WIDTH : (s + 2) * WIDTH]
 
     def other_products(ext, b):
-        taken = jnp.concatenate([ext[b + REACH - offsets[b, s]] for s in range(SLOTS)], axis=1)
+        taken = jnp.concatenate([ext[b + REACH - offsets[s, b]] for s in range(SLOTS)], axis=1)
         spread = [product[b + d, slot_of[b + d, d - 1]] for d in range(1, REACH + 1)]
         spread = (spread[0] + spread[1]) + (spread[2] + spread[3])
         out = mm3(taken, (high[b, :, WIDTH:], low[b, :, WIDTH:]), True)
         stiff_new[b] = stiff_new[b] + out + spread
 
-    def apply_stiffness(app, ready, hooks):
-        ext = exts[app]
-        ready(0)
-        for b in range(REACH):
-            own_products(ext, b)
+    def send_forward(app):
+        @pl.when(me < count - 1)
+        def _():
+            forward(app).start()
+
+    def send_backward(app):
         for e in range(REACH):
             out = jnp.zeros((MODES, WIDTH), jnp.float32)
             for b in range(e + 1):
                 out = out + product[b, slot_of[b, b - e + REACH - 1]]
             edge[app, e] = out
-        hooks[0]()
-
-        @pl.when(me < count - 1)
-        def _():
-            forward(app).start()
 
         @pl.when(me > 0)
         def _():
             backward(app).start()
 
+    def late_part(app, g):
+        return mm3(wide([(exts[app], REACH)], g), wide([(stiff_new, 0)], g), True)
+
+    def rest_of_product(app, ready):
+        ext = exts[app]
         for g in range(1, groups):
             ready(g)
             for b in range(g * REACH, (g + 1) * REACH):
                 own_products(ext, b)
-        hooks[1]()
         for b in range(REACH, blocks):
             other_products(ext, b)
+        acc = late_part(app, 1)
+        for g in range(2, groups - 1):
+            acc = acc + late_part(app, g)
 
         @pl.when(me > 0)
         def _():
@@ -353,6 +344,7 @@
 
         for b in range(REACH):
             other_products(ext, b)
+        acc = acc + late_part(app, 0)
 
         @pl.when(me < count - 1)
         def _():
@@ -360,6 +352,8 @@
             for k in range(REACH):
                 b = blocks - REACH + k
                 stiff_new[b] = stiff_new[b] + returned[app, k]
+
+        return acc + late_part(app, groups - 1)
 
     class Channel:
         def __init__(self, refs):
@@ -500,13 +494,6 @@
             [ref[group * REACH + k : group * REACH + k + 1, :] for k in range(REACH)], axis=1
         )
 
-    def late_block(app):
-        ext = exts[app]
-        acc = mm3(wide([(ext, REACH)], 0), wide([(stiff_new, 0)], 0), True)
-        for g in range(1, groups):
-            acc = acc + mm3(wide([(ext, REACH)], g), wide([(stiff_new, 0)], g), True)
-        return acc
-
     for b in range(blocks + REACH):
         product[b, SLOTS] = jnp.zeros((MODES, WIDTH), jnp.float32)
     for copy in loads:
@@ -521,7 +508,7 @@
         for d in range(1, REACH + 1):
             slot = SLOTS
             for s in range(SLOTS):
-                slot = jnp.where(offsets[b, s] == d, s, slot)
+                slot = jnp.where(offsets[s, b] == d, s, slot)
             slot_of[b, d - 1] = slot
     for b in range(blocks, blocks + REACH):
         for d in range(REACH):
@@ -534,12 +521,14 @@
             whole = jnp.concatenate([diag[b]] + [coupling[b, s] for s in range(SLOTS)], axis=1)
             high[b], low[b] = split(whole)
 
-    def enter():
-        pl.semaphore_wait(barrier, len(greeted))
-        channels[0][0].start()
-
-    apply_stiffness(0, ready, (enter, lambda: None))
-    channels[0][1].store(pack32(late_block(0)))
+    ready(0)
+    for b in range(REACH):
+        own_products(ext0, b)
+    pl.semaphore_wait(barrier, len(greeted))
+    send_forward(0)
+    send_backward(0)
+    channels[0][0].start()
+    channels[0][1].store(pack32(rest_of_product(0, ready)))
     channels[0][1].start()
     identity = eye(WIDTH)
     for b in range(blocks):
@@ -563,11 +552,11 @@
         n = MODES * (3 if moving else 2)
         stiff_acc = jnp.zeros((MODES, n - MODES), jnp.float32)
         mass_acc = jnp.zeros((MODES, n), jnp.float32)
-        for g in range(groups):
+        for g in (groups - 1, 0, *range(1, groups - 1)):
             new = mm3(both, wide(basis, g))
             stiff = mm3(both, wide(stiff_basis, g))
             masses = wide_row(mass, g)
-            residual = stiff[:MODES] - mm3(projected[:, :MODES], new[:MODES] * masses)
+            residual = stiff[:MODES] - mm3(projected, new[:MODES] * masses)
             residual = residual * wide_row(inverse_diag, g)
             for k in range(REACH):
                 b = g * REACH + k
@@ -581,23 +570,24 @@
             right = [new[:MODES], residual] + ([new[MODES:]] if moving else [])
             mass_acc = mass_acc + mm3(residual * masses, jnp.concatenate(right, axis=0), True)
             stiff_acc = stiff_acc + mm3(residual, stiff, True)
+            if g == 0:
+                for b in range(REACH):
+                    own_products(ext, b)
+                send_forward(step)
+                send_backward(step)
         mass_sum, stiff_sum, late_sum = channels[step]
         mass_sum.store(pack96(mass_acc) if moving else pack64(mass_acc))
         stiff_sum.store(pack64(stiff_acc) if moving else pack32(stiff_acc))
-
-        def leave(mass_sum=mass_sum, stiff_sum=stiff_sum):
-            mass_sum.start()
-            stiff_sum.start()
-
-        apply_stiffness(step, lambda g: None, (leave, lambda: None))
+        mass_sum.start()
+        stiff_sum.start()
+        late_sum.store(pack32(rest_of_product(step, lambda g: None)))
+        late_sum.start()
         basis = [(modes, 0), (ext, REACH)] + ([(direction, 0)] if moving else [])
         stiff_basis = [(stiff_modes, 0), (stiff_new, 0)] + ([(stiff_direction, 0)] if moving else [])
-        late_sum.store(pack32(late_block(step)))
-        late_sum.start()
         shape = (MODES, n)
         lane = lanes(shape)
         unit = jnp.where(lane == sublanes(shape), 1.0, 0.0)
-        placed = mm(0.5 * projected[:, :MODES], unit, HIGHEST)
+        placed = mm(0.5 * projected, unit, HIGHEST)
         third = []
         if moving:
             zero = jnp.zeros((MODES, order), jnp.float32)
@@ -631,7 +621,6 @@
         known = mm_nt(mm(factor, rest, HIGHEST), factor, HIGHEST)
         block = unpack32(late_sum.finish())
         reduced = known + mm_nt(mm(middle, block, HIGHEST), middle, HIGHEST)
-        reduced = 0.5 * (reduced + reduced.T)
         coefficients, projected = ritz_rows(reduced, factor)
         if step < ITERS:
             spot = jnp.where(lane == sublanes(shape) + MODES, 1.0, 0.0)
@@ -681,11 +670,11 @@
             lambda *refs: solve_kernel((count, blocks), *refs),
             out_shape=[jax.ShapeDtypeStruct((blocks, WIDTH), f32)] * 2,
             in_specs=[
-                pl.BlockSpec(memory_space=pl.ANY),
-                pl.BlockSpec(memory_space=pl.ANY),
-                pl.BlockSpec(memory_space=pl.ANY),
-                pl.BlockSpec(memory_space=pl.ANY),
-                pl.BlockSpec(memory_space=pl.ANY),
+                pl.BlockSpec(memory_space=pltpu.HBM),
+                pl.BlockSpec(memory_space=pltpu.HBM),
+                pl.BlockSpec(memory_space=pltpu.HBM),
+                pl.BlockSpec(memory_space=pltpu.HBM),
+                pl.BlockSpec(memory_space=pltpu.HBM),
             ],
             out_specs=[pl.BlockSpec(memory_space=pltpu.VMEM)] * 2,
             scratch_shapes=[
@@ -694,7 +683,7 @@
                 pltpu.VMEM((blocks, WIDTH, (SLOTS + 1) * WIDTH), jnp.bfloat16),
                 pltpu.VMEM((blocks, WIDTH, (SLOTS + 1) * WIDTH), jnp.bfloat16),
                 pltpu.VMEM((blocks, WIDTH), f32),
-                pltpu.SMEM((blocks, SLOTS), jnp.int32),
+                pltpu.SMEM((SLOTS, blocks), jnp.int32),
                 pltpu.SMEM((blocks + REACH, REACH), jnp.int32),
                 pltpu.VMEM((blocks, WIDTH), f32),
                 pltpu.VMEM((blocks + REACH, SLOTS + 1, MODES, WIDTH), f32),
@@ -717,10 +706,10 @@
                 *channel_shapes,
             ],
             compiler_params=pltpu.CompilerParams(
-                collective_id=0, has_side_effects=True, vmem_limit_bytes=60 << 20
+                collective_id=0, has_side_effects=True, vmem_limit_bytes=56 << 20
             ),
             name="lobpcg",
-        )(diag_blocks, coupling, offsets, mass.reshape(blocks, WIDTH), initial_modes)
+        )(diag_blocks, coupling, offsets.T, mass.reshape(blocks, WIDTH), initial_modes)
         return outs[0].reshape(-1), outs[1].reshape(-1)
 
     spec = ("sub", "row")

time: 138 us -> 123 us (0.89)
  Pallas kernels: 133 us -> 119 us
    pallas_call x1, Pallas kernels: 133 us -> 119 us  [local(): pl.pallas_call(lambda *refs: solve_kernel((count, blocks), *refs), out_sh...]
    unnamed x3 -> x2, local copies, waits for them, and re-layouts: 3.95 us -> 2.59 us
where the time goes in v4:
time: 123 us
  Pallas kernels  119 us (97%)
  local copies, waits for them, and re-layouts  2.59 us (2%)
    pallas_call x1, Pallas kernels, local(): pl.pallas_call(lambda *refs: solve_kernel((count, blocks), *refs), out_sh...  119 us
    unnamed x2, local copies, waits for them, and re-layouts  2.59 us

profile of v4, /device:TPU:513, one launch (start us, length us, event | category | flops | bytes accessed | tf_op | source)
XLA Modules:
  0.0 122.5 jit_solution(4021557348430177843)
XLA Ops:
  0.6 119.3 %lobpcg.1 = (f32[16,128]{1,0:T(8,128)}, f32[16,128]{1,0:T(8,128)}) custom-call(f32[16,128,128]{2,1,0:T(8,128)} %refs_0_.1, f32[16,3,128,128]{3,2,1,0:T(8,128)} %refs_1_.1, s32[3,16]{1,0:T(4,128)} %bitcast.7, f32[16,128]{1,0:T(8,128)} %bitcast.4, f32[32,2048]{1,0:T(8,128)} %refs_4_.1), custom_call_target="tpu_custom_call" | custom-call | tf_op jit(solution)/shard_map/lobpcg/pallas_call | solution.py:669
  119.9 1.3 %copy.9 = f32[2048]{0:T(1024)} copy(f32[2048]{0:T(1024)} %bitcast.6) | data formatting | bytes 16384
  121.2 1.3 %copy.10 = f32[2048]{0:T(1024)} copy(f32[2048]{0:T(1024)} %bitcast.5) | data formatting | bytes 16384

commit v5 on v4

--- a/solution.py
+++ b/solution.py
@@ -66,30 +66,54 @@
     return jnp.sum(jnp.sum(x, axis=0, keepdims=True), axis=1, keepdims=True)
 
 
-def inverse_factor(table, first):
+def inverse_factor(table, first, halfway=lambda: None):
     rows, cols = table.shape
+    index = sublanes((8, cols))
+    lane = lanes((1, cols))
     done = []
+    below = table
     for start in range(0, rows, 8):
-        live = table.shape[0]
-        column = [
-            jnp.broadcast_to(table[:, first + start + k : first + start + k + 1], (live, cols))
+        if start == rows // 2:
+            halfway()
+        at = first + start
+        top, below = below[:8], below[8:]
+        parts = [top] + ([below] if below.shape[0] else [])
+        columns = [
+            [jnp.broadcast_to(part[:, at + k : at + k + 1], part.shape) for part in parts]
             for k in range(8)
         ]
-        index = sublanes((live, cols))
-        lane = lanes((live, cols))
-        for k in range(8):
-            at = first + start + k
-            pivot = column[k][k : k + 1, :]
-            scale = lax.rsqrt(pivot)
-            row = jnp.where(lane[0:1] == at, 1.0, table[k : k + 1, :]) * scale
-            factor = jnp.where(index > k, column[k] * scale, 0.0)
-            table = jnp.where((index > k) & (lane == at), 0.0, table) - factor * row
-            table = jnp.where(index == k, row, table)
-            for m in range(k + 1, 8):
-                column[m] = column[m] - factor * (column[m][k : k + 1, :] * scale)
-        done.append(table[:8])
-        table = table[8:]
-    result = jnp.concatenate(done, axis=0) if len(done) > 1 else done[0]
+        panel = (lane >= at) & (lane < at + 8)
+        parts = [jnp.where(panel, 0.0, part) for part in parts]
+        for k in range(0, 8, 2):
+            one, two = columns[k], columns[k + 1]
+            a, c = one[0][k : k + 1, :], two[0][k + 1 : k + 2, :]
+            b = one[0][k + 1 : k + 2, :]
+            scale = lax.rsqrt(a)
+            rest = lax.rsqrt(a * c - b * b)
+            scale_two = a * scale * rest
+            cross = b * scale * rest
+            row = (parts[0][k : k + 1, :] + jnp.where(lane == at + k, 1.0, 0.0)) * scale
+            row_two = (
+                parts[0][k + 1 : k + 2, :] + jnp.where(lane == at + k + 1, 1.0, 0.0)
+            ) * scale_two - cross * (parts[0][k : k + 1, :] + jnp.where(lane == at + k, 1.0, 0.0))
+            factors = [column * scale for column in one]
+            factors_two = [q * scale_two - p * cross for p, q in zip(one, two)]
+            factors[0] = jnp.where(index > k + 1, factors[0], 0.0)
+            factors_two[0] = jnp.where(index > k + 1, factors_two[0], 0.0)
+            parts = [
+                part - f * row - g * row_two for part, f, g in zip(parts, factors, factors_two)
+            ]
+            parts[0] = jnp.where(index == k, row, jnp.where(index == k + 1, row_two, parts[0]))
+            for m in range(k + 2, 8):
+                entry = columns[m][0][k : k + 1, :] * scale
+                entry_two = columns[m][0][k + 1 : k + 2, :] * scale_two - cross * columns[m][0][k : k + 1, :]
+                columns[m] = [
+                    c_ - f * entry - g * entry_two
+                    for c_, f, g in zip(columns[m], factors, factors_two)
+                ]
+        done.append(parts[0])
+        below = parts[-1]
+    result = jnp.concatenate(done, axis=0)
     shape = (rows, cols)
     return jnp.where(lanes(shape) <= sublanes(shape) + first, result, 0.0)
 
@@ -106,10 +130,29 @@
         MODES / jnp.maximum(highest - center, 1e-6), (n - MODES) / jnp.maximum(center - lowest, 1e-6)
     )
     initial = factor / n * (center * identity - matrix) + MODES / n * identity
+    edge = jnp.zeros((n, WIDTH - n), jnp.float32)
+    initial = jnp.concatenate([initial, edge], axis=1)
+    identity = jnp.where(lanes((n, WIDTH)) == sublanes((n, WIDTH)), 1.0, 0.0)
+    fill = jnp.zeros((WIDTH - n, WIDTH), jnp.bfloat16)
+    empty = jnp.zeros((WIDTH, WIDTH), jnp.bfloat16)
 
     def step(index, density):
-        square = mm3(density, density)
-        cube = mm3(square, density)
+        high, low = [jnp.concatenate([part, fill], axis=0) for part in split(density)]
+        weights = jnp.concatenate(
+            [jnp.concatenate([high, low], axis=1), jnp.concatenate([high, empty], axis=1)], axis=0
+        )
+
+        def times_density(value):
+            both = lax.dot_general(
+                jnp.concatenate(split(value), axis=1),
+                weights,
+                (((1,), (0,)), ((), ())),
+                preferred_element_type=jnp.float32,
+            )
+            return both[:, :WIDTH] + both[:, WIDTH:]
+
+        square = times_density(density)
+        cube = times_density(square)
         denominator = total((density - square) * identity)
         numerator = total(square * (identity - density))
         safe = jnp.where(jnp.abs(denominator) > 1e-12, denominator, 1.0)
@@ -120,7 +163,7 @@
         second = (1.0 + ratio) * scale
         return first * density + second * square - scale * cube
 
-    return lax.fori_loop(0, PURIFY, step, initial)
+    return lax.fori_loop(0, PURIFY, step, initial)[:MODES, :n]
 
 
 def pack32(block):
@@ -153,21 +196,21 @@
     return inverse_factor(0.5 * (gram_mass + gram_mass.T), 0)
 
 
-def next_factor(gram_mass):
+def next_factor(gram_mass, halfway):
     n = gram_mass.shape[0]
     rest = n - MODES
     side = gram_mass[:, :MODES]
     side = jnp.where(sublanes((n, MODES)) < MODES, 0.0, side)
     lower = gram_mass[MODES:, :]
     schur = lower - mm_nt(side[MODES:], side, HIGHEST)
-    bottom = inverse_factor(jnp.where(lanes((rest, n)) < MODES, -lower, schur), MODES)
+    bottom = inverse_factor(jnp.where(lanes((rest, n)) < MODES, -lower, schur), MODES, halfway)
     shape = (MODES, n)
     unit = jnp.where(lanes(shape) == sublanes(shape), 1.0, 0.0)
     return jnp.concatenate([unit, bottom], axis=0)
 
 
 def ritz_rows(reduced, factor):
-    rows = purify(reduced)[:MODES]
+    rows = purify(reduced)
     change = inverse_factor(mm_nt(rows, rows, HIGHEST), 0)
     coefficients = mm(rows, factor, HIGHEST)
     projected = mm_nt(mm(rows, reduced, HIGHEST), rows, HIGHEST)
@@ -183,8 +226,7 @@
     offsets_hbm,
     mass_hbm,
     initial_hbm,
-    mass_out,
-    energy_out,
+    out,
     diag,
     coupling,
     high,
@@ -610,34 +652,38 @@
         half = jnp.where((lane >= MODES) & (lane < 2 * MODES), 0.5, 1.0)
         gram_mass = jnp.concatenate([0.5 * unit, early_mass * half] + third[1], axis=0)
         gram_mass = gram_mass + gram_mass.T
-        factor = next_factor(gram_mass)
-        middle = factor[:, MODES : 2 * MODES]
-        early_stiff = stiff_sum.finish()
-        early_stiff = unpack64(early_stiff) if moving else unpack32(early_stiff)
+        arrived = []
+
+        def collect(arrived=arrived):
+            arrived.append(stiff_sum.finish())
+            arrived.append(late_sum.finish())
+
+        factor = next_factor(gram_mass, collect if moving else lambda: None)
+        if not moving:
+            collect()
+        early_stiff = unpack64(arrived[0]) if moving else unpack32(arrived[0])
+        block_lane = lanes((8, WIDTH))
+        here = (block_lane >= MODES) & (block_lane < 2 * MODES)
+        turned = [arrived[1] if k == 1 else pltpu.roll(arrived[1], (1 - k) % 4 * MODES, 1) for k in range(4)]
+        block = jnp.concatenate([jnp.where(here, 0.5 * t, 0.0) for t in turned], axis=0)[:, :n]
         empty = jnp.zeros((MODES, MODES), jnp.float32)
         pieces = [early_stiff[:, :MODES], empty] + ([early_stiff[:, MODES:]] if moving else [])
-        rest = jnp.concatenate([placed, jnp.concatenate(pieces, axis=1)] + third[0], axis=0)
-        rest = rest + rest.T
-        known = mm_nt(mm(factor, rest, HIGHEST), factor, HIGHEST)
-        block = unpack32(late_sum.finish())
-        reduced = known + mm_nt(mm(middle, block, HIGHEST), middle, HIGHEST)
+        gram_stiff = jnp.concatenate([placed, jnp.concatenate(pieces, axis=1) + block] + third[0], axis=0)
+        gram_stiff = gram_stiff + gram_stiff.T
+        reduced = mm_nt(mm(factor, gram_stiff, HIGHEST), factor, HIGHEST)
         coefficients, projected = ritz_rows(reduced, factor)
-        if step < ITERS:
-            spot = jnp.where(lane == sublanes(shape) + MODES, 1.0, 0.0)
-            inner = [jnp.zeros(shape, jnp.float32), mm(block, spot, HIGHEST)]
-            inner += [jnp.zeros(shape, jnp.float32)] * (n // MODES - 2)
-            previous = [rest + jnp.concatenate(inner, axis=0), gram_mass]
-
-    weight = count * blocks * WIDTH / MODES
+        previous = [gram_stiff, gram_mass]
+
     for g in range(groups):
         new = mm3(coefficients, wide(basis, g))
         stiff = mm3(coefficients, wide(stiff_basis, g))
-        density = weight * wide_row(mass, g) * jnp.sum(new * new, axis=0, keepdims=True)
-        energy = weight * jnp.sum(new * stiff, axis=0, keepdims=True)
+        squares = jnp.sum(new * new, axis=0, keepdims=True)
+        energy = jnp.sum(new * stiff, axis=0, keepdims=True)
         for k in range(REACH):
             cut = slice(k * WIDTH, (k + 1) * WIDTH)
-            mass_out[g * REACH + k : g * REACH + k + 1, :] = density[:, cut]
-            energy_out[g * REACH + k : g * REACH + k + 1, :] = energy[:, cut]
+            b = g * REACH + k
+            out[0, b : b + 1, :] = squares[:, cut]
+            out[1, b : b + 1, :] = energy[:, cut]
     drain(ITERS)
 
 
@@ -666,9 +712,9 @@
                     dma((side * cores,)),
                     dma((2, side)),
                 ]
-        outs = pl.pallas_call(
+        sums = pl.pallas_call(
             lambda *refs: solve_kernel((count, blocks), *refs),
-            out_shape=[jax.ShapeDtypeStruct((blocks, WIDTH), f32)] * 2,
+            out_shape=jax.ShapeDtypeStruct((2, blocks, WIDTH), f32),
             in_specs=[
                 pl.BlockSpec(memory_space=pltpu.HBM),
                 pl.BlockSpec(memory_space=pltpu.HBM),
@@ -676,7 +722,7 @@
                 pl.BlockSpec(memory_space=pltpu.HBM),
                 pl.BlockSpec(memory_space=pltpu.HBM),
             ],
-            out_specs=[pl.BlockSpec(memory_space=pltpu.VMEM)] * 2,
+            out_specs=pl.BlockSpec(memory_space=pltpu.VMEM),
             scratch_shapes=[
                 pltpu.VMEM((blocks, WIDTH, WIDTH), f32),
                 pltpu.VMEM((blocks, SLOTS, WIDTH, WIDTH), f32),
@@ -710,7 +756,8 @@
             ),
             name="lobpcg",
         )(diag_blocks, coupling, offsets.T, mass.reshape(blocks, WIDTH), initial_modes)
-        return outs[0].reshape(-1), outs[1].reshape(-1)
+        weight = count * blocks * WIDTH / MODES
+        return weight * mass * sums[0].reshape(-1), weight * sums[1].reshape(-1)
 
     spec = ("sub", "row")
     return jax.shard_map(

time: 123 us -> 122 us (level)
  other arithmetic: 0 us -> 2.6 us
  local copies, waits for them, and re-layouts: 2.59 us -> 0.01 us
    mul x0 -> x2, other arithmetic: none -> 2.6 us  [local(): return (weight * mass * sums[0].reshape(-1), weight * sums[1].reshape(-1))]
    unnamed x2, local copies, waits for them, and re-layouts: 2.59 us -> 0.01 us
where the time goes in v5:
time: 122 us
  Pallas kernels  119 us (98%)
  other arithmetic  2.6 us (2%)
    pallas_call x1, Pallas kernels, local(): pl.pallas_call(lambda *refs: solve_kernel((count, blocks), *refs), out_sh...  119 us
    mul x2, other arithmetic, local(): return (weight * mass * sums[0].reshape(-1), weight * sums[1].reshape(-1))  2.6 us

profile of v5, /device:TPU:513, one launch (start us, length us, event | category | flops | bytes accessed | tf_op | source)
XLA Modules:
  0.0 122.2 jit_solution(16994960853067805853)
XLA Ops:
  0.6 0.0 copy-start
  0.6 118.9 %lobpcg.1 = f32[2,16,128]{2,1,0:T(8,128)} custom-call(f32[16,128,128]{2,1,0:T(8,128)} %refs_0_.1, f32[16,3,128,128]{3,2,1,0:T(8,128)} %refs_1_.1, s32[3,16]{1,0:T(4,128)} %bitcast.7, f32[16,128]{1,0:T(8,128)} %bitcast.6, f32[32,2048]{1,0:T(8,128)} %refs_4_.1), custom_call_target="tpu_custom_call" | custom-call | tf_op jit(solution)/shard_map/lobpcg/pallas_call | solution.py:715
  119.6 1.3 %multiply_bitcast_fusion = f32[2048]{0:T(1024)} fusion(f32[2,16,128]{2,1,0:T(8,128)} %lobpcg.1), kind=kLoop, calls=%fused_computation.1 | loop fusion | flops 2048 | bytes 16384 | tf_op jit(solution)/shard_map/mul | solution.py:760
  120.9 0.0 copy-done
  120.9 1.3 %bitcast_multiply_fusion = f32[2048]{0:T(1024)} fusion(f32[2,16,128]{2,1,0:T(8,128)} %lobpcg.1, f32[2048]{0:T(1024)S(1)} %copy-done), kind=kLoop, calls=%fused_computation | loop fusion | flops 4096 | bytes 24576 | tf_op jit(solution)/shard_map/mul | solution.py:760
Async XLA Ops:
  0.6 120.2 %copy-start = (f32[2048]{0:T(1024)S(1)}, f32[2048]{0:T(1024)}, u32[]{:S(2)}) copy-start(f32[2048]{0:T(1024)} %param.8) | copy-start | bytes 24580

commit v6 on v5

--- a/solution.py
+++ b/solution.py
@@ -66,15 +66,13 @@
     return jnp.sum(jnp.sum(x, axis=0, keepdims=True), axis=1, keepdims=True)
 
 
-def inverse_factor(table, first, halfway=lambda: None):
+def inverse_factor(table, first):
     rows, cols = table.shape
     index = sublanes((8, cols))
     lane = lanes((1, cols))
     done = []
     below = table
     for start in range(0, rows, 8):
-        if start == rows // 2:
-            halfway()
         at = first + start
         top, below = below[:8], below[8:]
         parts = [top] + ([below] if below.shape[0] else [])
@@ -196,14 +194,14 @@
     return inverse_factor(0.5 * (gram_mass + gram_mass.T), 0)
 
 
-def next_factor(gram_mass, halfway):
+def next_factor(gram_mass):
     n = gram_mass.shape[0]
     rest = n - MODES
     side = gram_mass[:, :MODES]
     side = jnp.where(sublanes((n, MODES)) < MODES, 0.0, side)
     lower = gram_mass[MODES:, :]
     schur = lower - mm_nt(side[MODES:], side, HIGHEST)
-    bottom = inverse_factor(jnp.where(lanes((rest, n)) < MODES, -lower, schur), MODES, halfway)
+    bottom = inverse_factor(jnp.where(lanes((rest, n)) < MODES, -lower, schur), MODES)
     shape = (MODES, n)
     unit = jnp.where(lanes(shape) == sublanes(shape), 1.0, 0.0)
     return jnp.concatenate([unit, bottom], axis=0)
@@ -289,6 +287,7 @@
         for copy in pair:
             copy.start()
 
+    farthest = sorted(range(1, side), key=lambda k: -min(k, side - k))
     x_at = [lax.rem(x + k, nx) for k in range(side)]
     y_at = [lax.rem(y + k, ny) for k in range(side)]
 
@@ -462,7 +461,7 @@
 
         def start(self):
             self.first[self.own_first] = self.part[core]
-            for k in range(1, side):
+            for k in farthest:
                 for half in range(2):
                     self.first_send(half, k).start()
             self.first_partner().start()
@@ -475,7 +474,7 @@
             while len(values) > 1:
                 values = [p + q for p, q in zip(values[::2], values[1::2])]
             self.second[core, self.own_second] = values[0]
-            for k in range(1, side):
+            for k in farthest:
                 for pcore in range(cores):
                     self.second_send(pcore, k).start()
             self.second_partner().start()
@@ -652,27 +651,27 @@
         half = jnp.where((lane >= MODES) & (lane < 2 * MODES), 0.5, 1.0)
         gram_mass = jnp.concatenate([0.5 * unit, early_mass * half] + third[1], axis=0)
         gram_mass = gram_mass + gram_mass.T
-        arrived = []
-
-        def collect(arrived=arrived):
-            arrived.append(stiff_sum.finish())
-            arrived.append(late_sum.finish())
-
-        factor = next_factor(gram_mass, collect if moving else lambda: None)
-        if not moving:
-            collect()
-        early_stiff = unpack64(arrived[0]) if moving else unpack32(arrived[0])
-        block_lane = lanes((8, WIDTH))
-        here = (block_lane >= MODES) & (block_lane < 2 * MODES)
-        turned = [arrived[1] if k == 1 else pltpu.roll(arrived[1], (1 - k) % 4 * MODES, 1) for k in range(4)]
-        block = jnp.concatenate([jnp.where(here, 0.5 * t, 0.0) for t in turned], axis=0)[:, :n]
+        factor = next_factor(gram_mass)
+        middle = factor[:, MODES : 2 * MODES]
+        early_stiff = stiff_sum.finish()
+        early_stiff = unpack64(early_stiff) if moving else unpack32(early_stiff)
         empty = jnp.zeros((MODES, MODES), jnp.float32)
         pieces = [early_stiff[:, :MODES], empty] + ([early_stiff[:, MODES:]] if moving else [])
-        gram_stiff = jnp.concatenate([placed, jnp.concatenate(pieces, axis=1) + block] + third[0], axis=0)
-        gram_stiff = gram_stiff + gram_stiff.T
-        reduced = mm_nt(mm(factor, gram_stiff, HIGHEST), factor, HIGHEST)
+        rest = jnp.concatenate([placed, jnp.concatenate(pieces, axis=1)] + third[0], axis=0)
+        rest = rest + rest.T
+        known = mm_nt(mm(factor, rest, HIGHEST), factor, HIGHEST)
+        tile = late_sum.finish()
+        block = unpack32(tile)
+        reduced = known + mm_nt(mm(middle, block, HIGHEST), middle, HIGHEST)
         coefficients, projected = ritz_rows(reduced, factor)
-        previous = [gram_stiff, gram_mass]
+        if step < ITERS:
+            block_lane = lanes((8, WIDTH))
+            here = (block_lane >= MODES) & (block_lane < 2 * MODES)
+            turned = [tile if k == 1 else pltpu.roll(tile, (1 - k) % 4 * MODES, 1) for k in range(4)]
+            inner = jnp.concatenate([jnp.where(here, t, 0.0) for t in turned], axis=0)[:, :n]
+            empty = jnp.zeros((MODES, n), jnp.float32)
+            inner = jnp.concatenate([empty, inner] + [empty] * (n // MODES - 2), axis=0)
+            previous = [rest + inner, gram_mass]
 
     for g in range(groups):
         new = mm3(coefficients, wide(basis, g))

time: 122 us -> 121 us (level)
  Pallas kernels: 119 us -> 117 us
    pallas_call x1, Pallas kernels: 119 us -> 117 us  [local(): pl.pallas_call(lambda *refs: solve_kernel((count, blocks), *refs), out_sh...]
where the time goes in v6:
time: 121 us
  Pallas kernels  117 us (97%)
  other arithmetic  2.6 us (2%)
    pallas_call x1, Pallas kernels, local(): pl.pallas_call(lambda *refs: solve_kernel((count, blocks), *refs), out_sh...  117 us
    mul x2, other arithmetic, local(): return (weight * mass * sums[0].reshape(-1), weight * sums[1].reshape(-1))  2.6 us

profile of v6, /device:TPU:513, one launch (start us, length us, event | category | flops | bytes accessed | tf_op | source)
XLA Modules:
  0.0 120.6 jit_solution(14997680155287214891)
XLA Ops:
  0.6 0.0 copy-start
  0.6 117.3 %lobpcg.1 = f32[2,16,128]{2,1,0:T(8,128)} custom-call(f32[16,128,128]{2,1,0:T(8,128)} %refs_0_.1, f32[16,3,128,128]{3,2,1,0:T(8,128)} %refs_1_.1, s32[3,16]{1,0:T(4,128)} %bitcast.7, f32[16,128]{1,0:T(8,128)} %bitcast.6, f32[32,2048]{1,0:T(8,128)} %refs_4_.1), custom_call_target="tpu_custom_call" | custom-call | tf_op jit(solution)/shard_map/lobpcg/pallas_call | solution.py:714
  118.0 1.3 %multiply_bitcast_fusion = f32[2048]{0:T(1024)} fusion(f32[2,16,128]{2,1,0:T(8,128)} %lobpcg.1), kind=kLoop, calls=%fused_computation.1 | loop fusion | flops 2048 | bytes 16384 | tf_op jit(solution)/shard_map/mul | solution.py:759
  119.3 0.0 copy-done
  119.3 1.3 %bitcast_multiply_fusion = f32[2048]{0:T(1024)} fusion(f32[2,16,128]{2,1,0:T(8,128)} %lobpcg.1, f32[2048]{0:T(1024)S(1)} %copy-done), kind=kLoop, calls=%fused_computation | loop fusion | flops 4096 | bytes 24576 | tf_op jit(solution)/shard_map/mul | solution.py:759
Async XLA Ops:
  0.6 118.7 %copy-start = (f32[2048]{0:T(1024)S(1)}, f32[2048]{0:T(1024)}, u32[]{:S(2)}) copy-start(f32[2048]{0:T(1024)} %param.8) | copy-start | bytes 24580

commit v7 on v6

--- a/solution.py
+++ b/solution.py
@@ -13,7 +13,7 @@
 WIDTH = 128
 TORUS = (8, 8, 2)
 MESH = pl.DeviceIdType.MESH
-CHANNELS = ((1, 1), (2, 1, 1), (3, 2, 1), (3, 2, 1))
+CHANNELS = ((1, 1), (3, 1), (5, 1), (5, 1))
 
 HIGHEST = lax.Precision.HIGHEST
 
@@ -616,11 +616,10 @@
                     own_products(ext, b)
                 send_forward(step)
                 send_backward(step)
-        mass_sum, stiff_sum, late_sum = channels[step]
-        mass_sum.store(pack96(mass_acc) if moving else pack64(mass_acc))
-        stiff_sum.store(pack64(stiff_acc) if moving else pack32(stiff_acc))
-        mass_sum.start()
-        stiff_sum.start()
+        early_sum, late_sum = channels[step]
+        packed = [pack96(mass_acc), pack64(stiff_acc)] if moving else [pack64(mass_acc), pack32(stiff_acc)]
+        early_sum.store(jnp.concatenate(packed, axis=0))
+        early_sum.start()
         late_sum.store(pack32(rest_of_product(step, lambda g: None)))
         late_sum.start()
         basis = [(modes, 0), (ext, REACH)] + ([(direction, 0)] if moving else [])
@@ -643,18 +642,16 @@
         else:
             third = [[], []]
         drain(step - 1)
-        mass_sum.middle()
-        stiff_sum.middle()
+        early_sum.middle()
         late_sum.middle()
-        early_mass = mass_sum.finish()
-        early_mass = unpack96(early_mass) if moving else unpack64(early_mass)
+        early = early_sum.finish()
+        early_mass = unpack96(early[:24]) if moving else unpack64(early[:16])
         half = jnp.where((lane >= MODES) & (lane < 2 * MODES), 0.5, 1.0)
         gram_mass = jnp.concatenate([0.5 * unit, early_mass * half] + third[1], axis=0)
         gram_mass = gram_mass + gram_mass.T
         factor = next_factor(gram_mass)
         middle = factor[:, MODES : 2 * MODES]
-        early_stiff = stiff_sum.finish()
-        early_stiff = unpack64(early_stiff) if moving else unpack32(early_stiff)
+        early_stiff = unpack64(early[24:]) if moving else unpack32(early[16:])
         empty = jnp.zeros((MODES, MODES), jnp.float32)
         pieces = [early_stiff[:, :MODES], empty] + ([early_stiff[:, MODES:]] if moving else [])
         rest = jnp.concatenate([placed, jnp.concatenate(pieces, axis=1)] + third[0], axis=0)

time: 121 us -> 120 us (level)
  no operation moved by 1% of the time
where the time goes in v7:
time: 120 us
  Pallas kernels  116 us (97%)
  other arithmetic  2.6 us (2%)
    pallas_call x1, Pallas kernels, local(): pl.pallas_call(lambda *refs: solve_kernel((count, blocks), *refs), out_sh...  116 us
    mul x2, other arithmetic, local(): return (weight * mass * sums[0].reshape(-1), weight * sums[1].reshape(-1))  2.6 us

profile of v7, /device:TPU:513, one launch (start us, length us, event | category | flops | bytes accessed | tf_op | source)
XLA Modules:
  0.0 119.7 jit_solution(13373980600717301435)
XLA Ops:
  0.6 0.0 copy-start
  0.6 116.5 %lobpcg.1 = f32[2,16,128]{2,1,0:T(8,128)} custom-call(f32[16,128,128]{2,1,0:T(8,128)} %refs_0_.1, f32[16,3,128,128]{3,2,1,0:T(8,128)} %refs_1_.1, s32[3,16]{1,0:T(4,128)} %bitcast.7, f32[16,128]{1,0:T(8,128)} %bitcast.6, f32[32,2048]{1,0:T(8,128)} %refs_4_.1), custom_call_target="tpu_custom_call" | custom-call | tf_op jit(solution)/shard_map/lobpcg/pallas_call | solution.py:711
  117.1 1.3 %multiply_bitcast_fusion = f32[2048]{0:T(1024)} fusion(f32[2,16,128]{2,1,0:T(8,128)} %lobpcg.1), kind=kLoop, calls=%fused_computation.1 | loop fusion | flops 2048 | bytes 16384 | tf_op jit(solution)/shard_map/mul | solution.py:756
  118.4 0.0 copy-done
  118.4 1.3 %bitcast_multiply_fusion = f32[2048]{0:T(1024)} fusion(f32[2,16,128]{2,1,0:T(8,128)} %lobpcg.1, f32[2048]{0:T(1024)S(1)} %copy-done), kind=kLoop, calls=%fused_computation | loop fusion | flops 4096 | bytes 24576 | tf_op jit(solution)/shard_map/mul | solution.py:756
Async XLA Ops:
  0.6 117.8 %copy-start = (f32[2048]{0:T(1024)S(1)}, f32[2048]{0:T(1024)}, u32[]{:S(2)}) copy-start(f32[2048]{0:T(1024)} %param.8) | copy-start | bytes 24580
